TPU v7x, 256 devices: a whole 4x4x8 slice. The times are simulated.
256 devices in a mesh: head: 4 (over z_hi, core), ctx: 64 (over y, z_lo, x).
Axes of the slice: x: 4, y: 4, z: 8 (z_hi: 2, z_lo: 4; z = z_hi * 4 + z_lo), core: 2. Of those that a mesh axis runs over, the one named last changes fastest.
Arguments:
- queries: bfloat16 [32768, 4096], P(('ctx', 'head')), may hold values from -66 to 66
- keys: bfloat16 [32768, 4096], P(('ctx', 'head')), may hold values from -6.6 to 6.6
- values: bfloat16 [32768, 4096], P(('ctx', 'head')), may hold values from -10 to 10
- w_gate: bfloat16 [8, 512, 512], P('head'), may hold values from -0.25 to 0.25
- w_up: bfloat16 [8, 512, 512], P('head'), may hold values from -0.25 to 0.25
- w_out: bfloat16 [8, 512, 512], P('head'), may hold values from -0.25 to 0.25
Outputs:
- mixed: bfloat16 [32768, 4096], P(('ctx', 'head'))
All inputs are finite; a program needn't handle non-finite values.
Results may differ from a plain program's by a relative error of at most 0.0072.
Values may be sent and summed in bfloat16 or wider, within the bound.
A program may use at most 128 MiB of HBM per device.

v0:
```python
import jax
import jax.numpy as jnp
from jax import lax
from jax.sharding import Mesh
from jax.sharding import PartitionSpec as P

HD = 512
WIN = 512
CTX = ("ctx_0", "ctx_1", "ctx_2")
CTX_HEAD = ("ctx_0", "ctx_1", "ctx_2", "head")


step_size = 0.02
epsilon = 1e-06


def extended(value, sides, width):
    for axis, dim in sides:
        count, length = (lax.axis_size(axis), value.shape[dim])
        up = [(i, (i + 1) % count) for i in range(count - 1)]
        down = [(j, i) for i, j in up]
        last = lax.slice_in_dim(value, length - width, length, axis=dim)
        first = lax.slice_in_dim(value, 0, width, axis=dim)
        before = lax.ppermute(last, axis, up)
        after = lax.ppermute(first, axis, down)
        value = jnp.concatenate([before, value, after], axis=dim)
    return value


def sum_in_order(pieces, axes, order):
    lengths = [lax.axis_size(a) for a in axes]
    pieces = pieces.reshape(*lengths, *pieces.shape[1:])
    pieces = pieces.transpose(*order, *range(len(axes), pieces.ndim))
    pieces = pieces.reshape(-1, *pieces.shape[len(axes) :])
    for k in order:
        pieces = lax.psum_scatter(pieces, axes[k], scatter_dimension=0, tiled=True)
    return pieces[0]


def split_up(value, dim, count):
    before, after = (value.shape[:dim], value.shape[dim + 1 :])
    return jnp.moveaxis(value.reshape(*before, count, -1, *after), dim, 0)


def sum_by_axis(value, axes, order, dim):
    count = lax.axis_size(axes)
    return sum_in_order(split_up(value, dim, count), axes, order)


def over_pieces(value, axis):
    return lax.all_gather(value, axis).sum(0)


def silu_pair(inputs):
    sigmoid = jax.nn.sigmoid(inputs)
    return (inputs * sigmoid, sigmoid * (1.0 + inputs * (1.0 - sigmoid)))


def window_block(query_block, key_block, value_block, first_row, total_rows):
    block_rows = query_block.shape[0]
    key_span = key_block.shape[0]
    scores = jnp.einsum(
        "qhd,khd->hqk", query_block, key_block, preferred_element_type=jnp.float32
    ) * HD ** (-0.5)
    query_place = first_row + jnp.arange(block_rows, dtype=jnp.int32)
    key_place = first_row - WIN + jnp.arange(key_span, dtype=jnp.int32)
    distance = query_place[:, None] - key_place[None, :]
    allowed = (
        (jnp.abs(distance) <= WIN) & (key_place[None, :] >= 0) & (key_place[None, :] < total_rows)
    )
    masked = jnp.where(allowed[None], scores, -1e30)
    largest = jnp.max(masked, axis=2, keepdims=True)
    weights = jnp.where(allowed[None], jnp.exp(masked - largest), 0.0)
    weights = (weights / jnp.sum(weights, axis=2, keepdims=True)).astype(jnp.bfloat16)
    return jnp.einsum("hqk,khd->qhd", weights, value_block, preferred_element_type=jnp.float32)


def window_attention(queries, key_padded, value_padded, first_row, total_rows, head_count):
    row_count = queries.shape[0]
    block_count = 1
    block_count = 1
    block_rows = row_count // block_count

    def one_block(index):
        offset_row = index * block_rows
        query_block = queries.reshape(block_rows, head_count, HD)
        key_block = key_padded.reshape(block_rows + 2 * WIN, head_count, HD)
        value_block = value_padded.reshape(block_rows + 2 * WIN, head_count, HD)
        return window_block(query_block, key_block, value_block, first_row + offset_row, total_rows)

    result = lax.map(one_block, jnp.arange(block_count, dtype=jnp.int32))
    return result.reshape(row_count, head_count * HD)


def per_device(queries, keys, values, w_gate, w_up, w_out):
    local_queries, local_keys, local_values = (
        lax.all_to_all(queries, "head", split_axis=1, concat_axis=0, tiled=True),
        lax.all_to_all(keys, "head", split_axis=1, concat_axis=0, tiled=True),
        lax.all_to_all(values, "head", split_axis=1, concat_axis=0, tiled=True),
    )
    row_count = local_queries.shape[0]
    feature_width = local_queries.shape[1]
    head_count = feature_width // HD
    joined = jnp.concatenate((local_keys, local_values), axis=1)
    padded = extended(joined, ((CTX, 0),), WIN)
    first_row = lax.axis_index(CTX) * row_count
    total_rows = row_count * lax.axis_size(CTX)
    attended = window_attention(
        local_queries,
        padded[:, :feature_width],
        padded[:, feature_width:],
        first_row,
        total_rows,
        head_count,
    )
    query_heads = local_queries.reshape(row_count, head_count, HD)
    key_heads = local_keys.reshape(row_count, head_count, HD)
    value_heads = local_values.reshape(row_count, head_count, HD)
    gate_pre = jnp.einsum("thd,hde->hte", key_heads, w_gate, preferred_element_type=jnp.float32)
    up_pre = jnp.einsum("thd,hde->hte", key_heads, w_up, preferred_element_type=jnp.float32)
    active, slopes = silu_pair(gate_pre)
    hidden = (active * up_pre).astype(jnp.bfloat16)
    backward = -jnp.einsum("the,hde->htd", value_heads, w_out, preferred_element_type=jnp.float32)
    gate_input = (backward * up_pre * slopes).astype(jnp.bfloat16)
    up_input = (backward * active).astype(jnp.bfloat16)
    grad_gate = jnp.einsum(
        "thd,hte->hde", key_heads, gate_input, preferred_element_type=jnp.float32
    )
    grad_up = jnp.einsum("thd,hte->hde", key_heads, up_input, preferred_element_type=jnp.float32)
    grad_out = -jnp.einsum("htd,the->hde", hidden, value_heads, preferred_element_type=jnp.float32)
    gradients = jnp.stack((grad_gate, grad_up, grad_out)).reshape(3 * head_count * HD, HD)
    weights_flat = jnp.stack((w_gate, w_up, w_out)).reshape(3 * head_count * HD, HD)
    share_rows = gradients.shape[0] // lax.axis_size(CTX)
    shared_sum = sum_by_axis(gradients, CTX, (0, 2, 1), 0)
    start_here = lax.axis_index(CTX) * share_rows
    block_ids = (start_here + jnp.arange(share_rows, dtype=jnp.int32)) // HD
    member = (block_ids[:, None] == jnp.arange(3 * head_count, dtype=jnp.int32)[None, :]).astype(
        jnp.float32
    )
    row_squares = jnp.sum(shared_sum * shared_sum, axis=1)
    partial_sums = jnp.dot(row_squares, member, precision=lax.Precision.HIGHEST)
    totals = over_pieces(partial_sums, CTX)
    inverse = lax.rsqrt(totals / (HD * HD) + epsilon)
    row_inverse = jnp.dot(member, inverse, precision=lax.Precision.HIGHEST)
    weight_rows = lax.dynamic_slice_in_dim(weights_flat, start_here, share_rows, 0).astype(
        jnp.float32
    )
    new_rows = (weight_rows - step_size * row_inverse[:, None] * shared_sum).astype(jnp.bfloat16)
    updated = lax.all_gather(new_rows, CTX, axis=0, tiled=True)
    updated = updated.reshape(3, head_count, HD, HD)
    query_gate = jnp.einsum(
        "thd,hde->hte", query_heads, updated[0], preferred_element_type=jnp.float32
    )
    query_up = jnp.einsum(
        "thd,hde->hte", query_heads, updated[1], preferred_element_type=jnp.float32
    )
    query_hidden = (jax.nn.silu(query_gate) * query_up).astype(jnp.bfloat16)
    learned = jnp.einsum(
        "htd,hde->the", query_hidden, updated[2], preferred_element_type=jnp.float32
    )
    mixed = (
        (attended.reshape(row_count, head_count, HD) + learned)
        .astype(jnp.bfloat16)
        .reshape(row_count, feature_width)
    )
    return lax.all_to_all(mixed, "head", split_axis=0, concat_axis=1, tiled=True)


def solution(mesh):
    split = Mesh(
        mesh.devices.reshape(mesh.shape["head"], 4, 4, 4), ("head", "ctx_0", "ctx_1", "ctx_2")
    )
    placed = (
        P(CTX_HEAD, None),
        P(CTX_HEAD, None),
        P(CTX_HEAD, None),
        P("head", None, None),
        P("head", None, None),
        P("head", None, None),
    )
    return jax.shard_map(
        per_device, mesh=split, in_specs=placed, out_specs=P(CTX_HEAD, None), check_vma=False
    )
```

profile of v0, /device:TPU:1, one launch (start us, length us, event | category | flops | bytes accessed | tf_op | source)
XLA Modules:
  0.0 800.7 jit_solution(17989401678173476783)
XLA Ops:
  6.5 2.4 copy.118
  8.9 9.9 %all-to-all-start = ((bf16[128,4,1024]{2,0,1:T(8,128)(2,1)}), bf16[128,4,1024]{2,0,1:T(8,128)(2,1)S(1)}, u32[]{:S(2)}, u32[]{:S(2)}) async-start(bf16[128,4,1024]{2,0,1:T(8,128)(2,1)} %bitcast.110), calls=%async_computation | async-start | bytes 2097152 | tf_op jit(solution)/shard_map/all_to_all | solution.py:98
  19.9 18.5 %all-to-all-done = bf16[128,4,1024]{2,0,1:T(8,128)(2,1)S(1)} async-done(((bf16[128,4,1024]{2,0,1:T(8,128)(2,1)}), bf16[128,4,1024]{2,0,1:T(8,128)(2,1)S(1)}, u32[]{:S(2)}, u32[]{:S(2)}) %all-to-all-start) | async-done | bytes 1048608 | tf_op jit(solution)/shard_map/all_to_all | solution.py:98
  38.5 12.6 %all-to-all-start.1 = ((bf16[128,4,1024]{2,0,1:T(8,128)(2,1)}), bf16[128,4,1024]{2,0,1:T(8,128)(2,1)S(1)}, u32[]{:S(2)}, u32[]{:S(2)}) async-start(bf16[128,4,1024]{2,0,1:T(8,128)(2,1)} %bitcast.109), calls=%async_computation.1 | async-start | bytes 2097152 | tf_op jit(solution)/shard_map/all_to_all | solution.py:99
  51.1 1.6 reshape.153
  52.6 2.4 copy.71
  55.1 13.5 %all-to-all-done.1 = bf16[128,4,1024]{2,0,1:T(8,128)(2,1)S(1)} async-done(((bf16[128,4,1024]{2,0,1:T(8,128)(2,1)}), bf16[128,4,1024]{2,0,1:T(8,128)(2,1)S(1)}, u32[]{:S(2)}, u32[]{:S(2)}) %all-to-all-start.1) | async-done | bytes 1048608 | tf_op jit(solution)/shard_map/all_to_all | solution.py:99
  68.6 1.6 reshape.152
  70.2 2.1 fusion.55
  77.6 1.4 pad_maximum_fusion.1
  79.0 3.3 copy.75
  82.4 76.0 %reduce-scatter.4.cloned.1.call-done = f32[16,48,512]{2,1,0:T(8,128)} async-done(((f32[64,48,512]{2,1,0:T(8,128)}), f32[16,48,512]{2,1,0:T(8,128)}) %reduce-scatter.4.cloned.1.call-update) | async-done | bytes 1572880 | tf_op jit(solution)/shard_map/reduce_scatter | solution.py:36
  158.5 29.7 %reduce-scatter.6.cloned.1.call-done = f32[4,48,512]{2,1,0:T(8,128)} async-done(((f32[16,48,512]{2,1,0:T(8,128)}), f32[4,48,512]{2,1,0:T(8,128)}) %reduce-scatter.6.cloned.1.call-update) | async-done | bytes 393232 | tf_op jit(solution)/shard_map/reduce_scatter | solution.py:36
  189.5 3.5 pad_maximum_fusion.2
  193.0 22.2 %reduce-scatter.8.cloned.1.call-done = f32[1,48,512]{2,1,0:T(8,128)} async-done(((f32[4,48,512]{2,1,0:T(8,128)}), f32[1,48,512]{2,1,0:T(8,128)}) %reduce-scatter.8.cloned.1.call-update) | async-done | bytes 98320 | tf_op jit(solution)/shard_map/reduce_scatter | solution.py:36
  216.6 159.5 %all-reduce = f32[384]{0:T(512)S(1)} all-reduce(f32[384]{0:T(512)S(1)} %dynamic-update-slice), channel_id=2, replica_groups=mesh['head'=4,'ctx_0'=4,'ctx_1'=4,'ctx_2'=4] {'ctx_0','ctx_1','ctx_2'}, use_global_device_ids=true, to_apply=%add | all-reduce | flops 384 | bytes 3072
  376.5 1.6 fusion.30
  379.2 1.5 pad_maximum_fusion.3
  382.0 5.3 collective-permute-start
  388.4 37.1 %all-to-all-start.2 = ((bf16[128,4,1024]{2,0,1:T(8,128)(2,1)}), bf16[128,4,1024]{2,0,1:T(8,128)(2,1)S(1)}, u32[]{:S(2)}, u32[]{:S(2)}) async-start(bf16[128,4,1024]{2,0,1:T(8,128)(2,1)} %bitcast.118), calls=%async_computation.2 | async-start | bytes 2097152 | tf_op jit(solution)/shard_map/all_to_all | solution.py:97
  425.5 2.4 fusion.6
  427.9 16.2 %all-to-all-done.2 = bf16[128,4,1024]{2,0,1:T(8,128)(2,1)S(1)} async-done(((bf16[128,4,1024]{2,0,1:T(8,128)(2,1)}), bf16[128,4,1024]{2,0,1:T(8,128)(2,1)S(1)}, u32[]{:S(2)}, u32[]{:S(2)}) %all-to-all-start.2) | async-done | bytes 1048608 | tf_op jit(solution)/shard_map/all_to_all | solution.py:97
  444.0 1.6 reshape.150
  445.6 16.3 %pad_maximum_fusion = bf16[1536,2048]{0,1:T(8,128)(2,1)S(1)} fusion(bf16[512,2048]{0,1:T(8,128)(2,1)} %collective-permute-done.1, bf16[512,1024]{0,1:T(8,128)(2,1)S(1)} %copy.94, bf16[512,1024]{0,1:T(8,128)(2,1)S(1)} %copy.93, bf16[512,2048]{0,1:T(8,128)(2,1)} %collective-permute-done), kind=kLoop, calls=%fused_computation.1 | loop fusion | flops 25165824 | bytes 12582912 | tf_op jit(solution)/shard_map/concatenate | solution.py:26
  462.0 3.0 fusion.48
  465.0 9.0 %fusion.50 = (f32[2,512]{1,0:T(2,128)S(1)}, f32[2,512,1536]{1,2,0:T(8,128)}) fusion(pred[512,1536]{0,1:T(8,128)(4,1)S(1)} %copy-done.7, bf16[1536,2,512]{0,2,1:T(8,128)(2,1)} %bitcast.126, bf16[512,2,512]{2,1,0:T(2,128)(2,1)S(1)} %copy-done), kind=kOutput, calls=%fused_computation.81 | convolution fusion | flops 1618478592 | bytes 11276288 | tf_op jit(solution)/shard_map/while/body/eval_jaxpr/sub | solution.py:73
  474.0 234.1 %all-gather.3.cloned.1.call-done = bf16[3072,512]{1,0:T(8,128)(2,1)} async-done(((bf16[48,512]{1,0:T(8,128)(2,1)}), bf16[3072,512]{1,0:T(8,128)(2,1)}) %all-gather.3.cloned.1.call-update) | async-done | bytes 3145744 | tf_op jit(solution)/shard_map/all_gather | solution.py:149
  708.1 3.0 fusion.49
  711.1 2.0 fusion.20
  713.2 4.8 fusion.14
  717.9 6.1 fusion.13
  724.5 68.4 %all_to_all.73 = bf16[4,128,1024]{1,2,0:T(8,128)(2,1)S(1)} all-to-all(bf16[4,128,1024]{1,2,0:T(8,128)(2,1)S(1)} %copy.83), channel_id=1, replica_groups=mesh['head'=4,'ctx_0'=4,'ctx_1'=4,'ctx_2'=4] {'head'}, dimensions={0} | all-to-all | bytes 2097152 | tf_op jit(solution)/shard_map/all_to_all | solution.py:166
  (53 shorter events, 14.1 us)
Async XLA Ops:
  6.5 12.3 %copy-start.5 = (bf16[128,4096]{1,0:T(8,128)(2,1)S(1)}, bf16[128,4096]{1,0:T(8,128)(2,1)}, u32[]{:S(2)}) copy-start(bf16[128,4096]{1,0:T(8,128)(2,1)} %param.8) | copy-start | bytes 3145732
  8.9 29.5 %all-to-all-start = ((bf16[128,4,1024]{2,0,1:T(8,128)(2,1)}), bf16[128,4,1024]{2,0,1:T(8,128)(2,1)S(1)}, u32[]{:S(2)}, u32[]{:S(2)}) async-start(bf16[128,4,1024]{2,0,1:T(8,128)(2,1)} %bitcast.110), calls=%async_computation | async-start | bytes 2097152 | tf_op jit(solution)/shard_map/all_to_all | solution.py:98
  38.5 30.2 %all-to-all-start.1 = ((bf16[128,4,1024]{2,0,1:T(8,128)(2,1)}), bf16[128,4,1024]{2,0,1:T(8,128)(2,1)S(1)}, u32[]{:S(2)}, u32[]{:S(2)}) async-start(bf16[128,4,1024]{2,0,1:T(8,128)(2,1)} %bitcast.109), calls=%async_computation.1 | async-start | bytes 2097152 | tf_op jit(solution)/shard_map/all_to_all | solution.py:99
  51.1 107.3 %reduce-scatter.4.cloned.1.call-start = ((), (), s32[]{:S(2)}) async-start(), calls=%async_computation.7 | async-start | bytes 7864320 | tf_op jit(solution)/shard_map/reduce_scatter | solution.py:36
  70.2 2.1 copy-start.3
  72.3 1.2 copy-start.1
  72.3 1.5 copy-start.4
  82.3 105.9 %copy-start.8 = (u32[256]{0:T(256)S(1)}, u32[256]{0:T(256)}, u32[]{:S(2)}) copy-start(u32[256]{0:T(256)} %constant.88) | copy-start | bytes 3076
  82.3 107.2 %copy-start.2 = (bf16[2,512,512]{2,1,0:T(8,128)(2,1)S(1)}, bf16[2,512,512]{2,1,0:T(8,128)(2,1)}, u32[]{:S(2)}) copy-start(bf16[2,512,512]{2,1,0:T(8,128)(2,1)} %param.10) | copy-start | bytes 3145732
  82.3 105.8 %reduce-scatter.6.cloned.1.call-start = ((), (), s32[]{:S(2)}) async-start(), calls=%async_computation.8 | async-start | bytes 1966080 | tf_op jit(solution)/shard_map/reduce_scatter | solution.py:36
  158.4 56.8 %reduce-scatter.8.cloned.1.call-start = ((), (), s32[]{:S(2)}) async-start(), calls=%async_computation.9 | async-start | bytes 491520 | tf_op jit(solution)/shard_map/reduce_scatter | solution.py:36
  188.2 519.9 %all-gather.3.cloned.1.call-start = ((), (), s32[]{:S(2)}) async-start(), calls=%async_computation.10 | async-start | bytes 3194880 | tf_op jit(solution)/shard_map/all_gather | solution.py:149
  379.2 8.1 %copy-start.6 = (bf16[128,4096]{1,0:T(8,128)(2,1)S(1)}, bf16[128,4096]{1,0:T(8,128)(2,1)}, u32[]{:S(2)}) copy-start(bf16[128,4096]{1,0:T(8,128)(2,1)} %param.6) | copy-start | bytes 3145732
  380.7 64.9 %collective-permute-start.1 = (bf16[512,2048]{0,1:T(8,128)(2,1)}, bf16[512,2048]{0,1:T(8,128)(2,1)}, u32[]{:S(2)}, u32[]{:S(2)}) collective-permute-start(bf16[512,2048]{0,1:T(8,128)(2,1)} %pad_maximum_fusion.3), channel_id=1, source_target_pairs={{1,0},{2,1},{3,2},{4,3},{5,4},{6,5},{7,6},{8,7},{9,8},{10,9},{11,1... | collective-permute-start | bytes 6291464 | tf_op jit(solution)/shard_map/ppermute | solution.py:25
  382.0 63.6 %collective-permute-start = (bf16[512,2048]{0,1:T(8,128)(2,1)}, bf16[512,2048]{0,1:T(8,128)(2,1)}, u32[]{:S(2)}, u32[]{:S(2)}) collective-permute-start(bf16[512,2048]{0,1:T(8,128)(2,1)} %pad_maximum_fusion.3), channel_id=1, source_target_pairs={{0,1},{1,2},{2,3},{3,4},{4,5},{5,6},{6,7},{7,8},{8,9},{9,10},{10,1... | collective-permute-start | bytes 6291464 | tf_op jit(solution)/shard_map/ppermute | solution.py:24
  388.4 55.6 %all-to-all-start.2 = ((bf16[128,4,1024]{2,0,1:T(8,128)(2,1)}), bf16[128,4,1024]{2,0,1:T(8,128)(2,1)S(1)}, u32[]{:S(2)}, u32[]{:S(2)}) async-start(bf16[128,4,1024]{2,0,1:T(8,128)(2,1)} %bitcast.118), calls=%async_computation.2 | async-start | bytes 2097152 | tf_op jit(solution)/shard_map/all_to_all | solution.py:97
  461.9 3.1 copy-start
  462.0 3.1 copy-start.7
Sparse Core Ops, SparseCore 0:
  82.4 75.9 reduce-scatter.3
  160.9 27.1 reduce-scatter.5
  190.7 24.5 reduce-scatter.7
  378.2 329.8 all-gather.2
where the time goes:
time: 801 us
  waiting for transfers between devices  410 us (51%)
  blocking collectives  228 us (28%)
  starting transfers between devices  66.3 us (8%)
  matrix products  28.9 us (4%)
  other arithmetic  27.8 us (3%)
  local copies, waits for them, and re-layouts  25.5 us (3%)
  between operations  14 us (2%)
    all_gather x1, waiting for transfers between devices, per_device(): updated = lax.all_gather(new_rows, CTX, axis=0, tiled=True)  234 us
    unnamed x1, blocking collectives  159 us
    reduce_scatter x3, waiting for transfers between devices, sum_in_order(): pieces = lax.psum_scatter(pieces, axes[k], scatter_dimension=0, tiled=True)  128 us
    all_to_all x1, blocking collectives, per_device(): lax.all_to_all(mixed, 'head', split_axis=0, concat_axis=1, tiled=True)  68.4 us
    all_to_all x1, starting transfers between devices, per_device(): lax.all_to_all(queries, 'head', split_axis=1, concat_axis=0, tiled=True)  37.1 us
    all_to_all x1, waiting for transfers between devices, per_device(): lax.all_to_all(keys, 'head', split_axis=1, concat_axis=0, tiled=True)  18.5 us
    concatenate x1, other arithmetic, extended(): value = jnp.concatenate([before, value, after], axis=dim)  16.3 us
    all_to_all x1, waiting for transfers between devices, per_device(): lax.all_to_all(queries, 'head', split_axis=1, concat_axis=0, tiled=True)  16.2 us
  transfers between devices with their start and end apart: 9, of which 7 were waited for; matrix products, arithmetic and copies ran while one was open for 6% of the time, Pallas kernels for 0%

commit v1 on v0

v1 whole, which is shorter than its diff:
```python
import functools

import jax
import jax.numpy as jnp
from jax import lax
from jax.experimental import pallas as pl
from jax.experimental.pallas import tpu as pltpu
from jax.sharding import Mesh
from jax.sharding import PartitionSpec as P

HD = 512
WIN = 512
Y, Z, X = "ctx_0", "ctx_1", "ctx_2"
CTX = (Y, Z, X)
CTX_HEAD = CTX + ("head",)
MESH = pl.DeviceIdType.MESH
STEP = 0.02
EPS = 1e-06
F32, BF16 = jnp.float32, jnp.bfloat16


def dot(a, b, dims=((1,), (0,))):
    return lax.dot_general(a, b, (dims, ((), ())), preferred_element_type=F32)


class Copies:
    def __init__(self, send_sem, recv_sem):
        self.send_sem, self.recv_sem, self.count, self.all = send_sem, recv_sem, 0, []

    def start(self, src, dst, axis, index):
        copy = pltpu.make_async_remote_copy(
            src_ref=src,
            dst_ref=dst,
            send_sem=self.send_sem.at[self.count],
            recv_sem=self.recv_sem.at[self.count],
            device_id={axis: index},
            device_id_type=MESH,
        )
        self.count += 1
        copy.start()
        self.all.append(copy)
        return copy


def ring(axis):
    me = lax.axis_index(axis)
    return me, lax.rem(me + 1, 4), lax.rem(me + 3, 4), lax.rem(me + 2, 4)


def rows(base, index, size, part=0, parts=1):
    step = size // parts
    return pl.ds(pl.multiple_of(base + index * size + part * step, 16), step)


class RingReduce:
    def __init__(self, copies, axis, buf, c, opp, side):
        self.copies, self.axis, self.buf, self.c, self.opp, self.side = copies, axis, buf, c, opp, side
        me, right, left, far = ring(axis)
        half = c // 2
        s = lambda src, dst, to: copies.start(src, dst, axis, to)
        self.far_r = s(buf.at[:, rows(0, far, c, 0, 2), :], opp.at[0], right)
        self.far_l = s(buf.at[:, rows(0, far, c, 1, 2), :], opp.at[1], left)
        self.near_r = s(buf.at[:, rows(0, right, c, 1, 2), :], side.at[0, :, pl.ds(half, half), :], right)
        self.near_l = s(buf.at[:, rows(0, left, c, 0, 2), :], side.at[1, :, pl.ds(0, half), :], left)

    def middle(self):
        me, right, left, far = ring(self.axis)
        c, buf, half = self.c, self.buf, self.c // 2
        self.far_r.wait_recv()
        at = rows(0, right, c, 0, 2)
        buf[:, at, :] = (buf[:, at, :].astype(F32) + self.opp[0].astype(F32)).astype(BF16)
        self.last_r = self.copies.start(buf.at[:, at, :], self.side.at[0, :, pl.ds(0, half), :], self.axis, right)
        self.far_l.wait_recv()
        at = rows(0, left, c, 1, 2)
        buf[:, at, :] = (buf[:, at, :].astype(F32) + self.opp[1].astype(F32)).astype(BF16)
        self.last_l = self.copies.start(buf.at[:, at, :], self.side.at[1, :, pl.ds(half, half), :], self.axis, left)

    def end(self, out):
        me, right, left, far = ring(self.axis)
        for copy in (self.near_r, self.near_l, self.last_r, self.last_l):
            copy.wait_recv()
        own = self.buf[:, rows(0, me, self.c), :].astype(F32)
        out[...] = (own + self.side[0].astype(F32) + self.side[1].astype(F32)).astype(BF16)


class LineReduce:
    def __init__(self, copies, axis, buf, c, slots):
        me = lax.axis_index(axis)
        self.axis, self.buf, self.c, self.slots, self.sent = axis, buf, c, slots, []
        for d in (1, 2, 3):
            peer = lax.rem(me + d, 4)
            self.sent.append(copies.start(buf.at[:, rows(0, peer, c), :], slots.at[d - 1], axis, peer))

    def end(self):
        me = lax.axis_index(self.axis)
        total = self.buf[:, rows(0, me, self.c), :].astype(F32)
        for d in range(3):
            self.sent[d].wait_recv()
            total += self.slots[d].astype(F32)
        return total


class LineGather:
    def __init__(self, copies, axis, buf, base, c):
        me = lax.axis_index(axis)
        self.sent = []
        for d in (1, 2, 3):
            peer = lax.rem(me + d, 4)
            at = buf.at[:, rows(base, me, c), :]
            self.sent.append(copies.start(at, at, axis, peer))

    def end(self):
        for copy in self.sent:
            copy.wait_recv()


class RingGather:
    def __init__(self, copies, axis, buf, base, c):
        self.copies, self.axis, self.buf, self.base, self.c = copies, axis, buf, base, c
        me, right, left, far = ring(axis)
        low, high = (buf.at[:, rows(base, me, c, part, 2), :] for part in (0, 1))
        self.low_r = copies.start(low, low, axis, right)
        self.high_l = copies.start(high, high, axis, left)
        self.high_r = copies.start(high, high, axis, right)
        self.low_l = copies.start(low, low, axis, left)

    def middle(self):
        me, right, left, far = ring(self.axis)
        self.low_r.wait_recv()
        at = self.buf.at[:, rows(self.base, left, self.c, 0, 2), :]
        self.far_r = self.copies.start(at, at, self.axis, right)
        self.high_l.wait_recv()
        at = self.buf.at[:, rows(self.base, right, self.c, 1, 2), :]
        self.far_l = self.copies.start(at, at, self.axis, left)

    def end(self):
        for copy in (self.high_r, self.low_l, self.far_r, self.far_l):
            copy.wait_recv()


def fast_kernel(
    q_ref, k_ref, v_ref, wg_ref, wu_ref, wo_ref, out_ref,
    grad, opp1, side1, part2, opp2, side2, part3, slots, total, fresh, send_sem, recv_sem,
):
    barrier = pltpu.get_barrier_semaphore()
    for axis, offsets in ((X, (1, 3)), (Y, (1, 3)), (Z, (1, 2, 3))):
        for d in offsets:
            peer = lax.rem(lax.axis_index(axis) + d, 4)
            pl.semaphore_signal(barrier, inc=1, device_id={axis: peer}, device_id_type=MESH)

    copies = Copies(send_sem, recv_sem)
    order = ((X, Y), (Y, X))
    first = [None, None]
    for h in range(2):
        cols = pl.ds(h * HD, HD)
        k, v = k_ref[:, cols], v_ref[:, cols]
        a, b = dot(k, wg_ref[h]), dot(k, wu_ref[h])
        back = -dot(v, wo_ref[h], ((1,), (1,)))
        sig = jax.nn.sigmoid(a)
        act = a * sig
        hidden = (act * b).astype(BF16)
        da = (back * b * (sig * (1.0 + a * (1.0 - sig)))).astype(BF16)
        db = (back * act).astype(BF16)
        for m, g in enumerate(
            (dot(k, da, ((0,), (0,))), dot(k, db, ((0,), (0,))), -dot(hidden, v, ((0,), (0,))))
        ):
            grad[h, m, 0:HD, :] = g[:, 0:256].astype(BF16)
            grad[h, m, HD : 2 * HD, :] = g[:, 256:512].astype(BF16)
        if h == 0:
            pl.semaphore_wait(barrier, 7)
        first[h] = RingReduce(copies, order[h][0], grad.at[h], 256, opp1.at[h], side1.at[h])
    second, third, gather = [None, None], [None, None], [None, None]
    for h in range(2):
        first[h].middle()
    for h in range(2):
        first[h].end(part2.at[h])
        second[h] = RingReduce(copies, order[h][1], part2.at[h], 64, opp2.at[h], side2.at[h])
    for h in range(2):
        second[h].middle()
    for h in range(2):
        second[h].end(part3.at[h])
        third[h] = LineReduce(copies, Z, part3.at[h], 16, slots.at[h])
    bases = [lax.axis_index(order[h][0]) * 256 for h in range(2)]
    inner = [bases[h] + lax.axis_index(order[h][1]) * 64 for h in range(2)]
    for h in range(2):
        total[h, :, rows(inner[h], lax.axis_index(Z), 16), :] = third[h].end().astype(BF16)
        third[h] = LineGather(copies, Z, total.at[h], inner[h], 16)
    for h in range(2):
        third[h].end()
        gather[h] = RingGather(copies, order[h][1], total.at[h], bases[h], 64)
    for h in range(2):
        gather[h].middle()
    for h in range(2):
        gather[h].end()
        gather[h] = RingGather(copies, order[h][0], total.at[h], 0, 256)
    for h in range(2):
        gather[h].middle()
    for h in range(2):
        gather[h].end()
        for m, w_ref in enumerate((wg_ref, wu_ref, wo_ref)):
            g = total[h, m].astype(F32)
            scale = STEP * lax.rsqrt(jnp.sum(g * g) / (HD * HD) + EPS)
            for part in (0, 1):
                cols = pl.ds(part * 256, 256)
                piece = total[h, m, pl.ds(part * HD, HD), :].astype(F32)
                fresh[m, :, cols] = (w_ref[h, :, cols].astype(F32) - scale * piece).astype(BF16)
        cols = pl.ds(h * HD, HD)
        q = q_ref[:, cols]
        gate = dot(q, fresh[0])
        hid = (gate * jax.nn.sigmoid(gate) * dot(q, fresh[1])).astype(BF16)
        out_ref[:, cols] = dot(hid, fresh[2])
    for copy in copies.all:
        copy.wait_send()


def fast_weight(q, k, v, wg, wu, wo):
    vmem = pl.BlockSpec(memory_space=pltpu.VMEM)
    n_copies = 60
    return pl.pallas_call(
        fast_kernel,
        out_shape=jax.ShapeDtypeStruct((512, 1024), F32),
        in_specs=[vmem] * 6,
        out_specs=vmem,
        scratch_shapes=[
            pltpu.VMEM((2, 3, 1024, 256), BF16),
            pltpu.VMEM((2, 2, 3, 128, 256), BF16),
            pltpu.VMEM((2, 2, 3, 256, 256), BF16),
            pltpu.VMEM((2, 3, 256, 256), BF16),
            pltpu.VMEM((2, 2, 3, 32, 256), BF16),
            pltpu.VMEM((2, 2, 3, 64, 256), BF16),
            pltpu.VMEM((2, 3, 64, 256), BF16),
            pltpu.VMEM((2, 3, 3, 16, 256), BF16),
            pltpu.VMEM((2, 3, 1024, 256), BF16),
            pltpu.VMEM((3, HD, HD), BF16),
            pltpu.SemaphoreType.DMA((n_copies,)),
            pltpu.SemaphoreType.DMA((n_copies,)),
        ],
        compiler_params=pltpu.CompilerParams(
            collective_id=0, has_side_effects=True, vmem_limit_bytes=48 * 1024 * 1024
        ),
        cost_estimate=pl.CostEstimate(flops=40_000_000_000, bytes_accessed=10_000_000, transcendentals=0),
        name="fast_weight",
    )(q, k, v, wg, wu, wo)


def attend_kernel(q_ref, kp_ref, k_ref, kn_ref, vp_ref, v_ref, vn_ref, learned_ref, out_ref):
    block = (lax.axis_index(Y) * 4 + lax.axis_index(Z)) * 4 + lax.axis_index(X)
    has_before, has_after = block > 0, block < 63
    r = lax.broadcasted_iota(jnp.int32, (256, 256), 0)
    c = lax.broadcasted_iota(jnp.int32, (256, 256), 1)
    for h in range(2):
        cols = pl.ds(h * HD, HD)
        for t in range(2):
            top = pl.ds(t * 256, 256)
            q = q_ref[top, cols]
            before = pl.ds(t * 256, 512 - t * 256)
            after = pl.ds(0, 256 + t * 256)
            sb = dot(q, kp_ref[before, cols], ((1,), (1,))) * HD**-0.5
            so = dot(q, k_ref[:, cols], ((1,), (1,))) * HD**-0.5
            sa = dot(q, kn_ref[after, cols], ((1,), (1,))) * HD**-0.5
            edge_b = jnp.where((c >= r) & has_before, sb[:, :256], -1e30)
            edge_a = jnp.where((c <= r) & has_after, sa[:, t * 256 :], -1e30)
            if t == 0:
                pieces = [edge_b, jnp.where(has_before, sb[:, 256:], -1e30), so, edge_a]
            else:
                pieces = [edge_b, so, jnp.where(has_after, sa[:, :256], -1e30), edge_a]
            s = jnp.concatenate(pieces, axis=1)
            s = jnp.exp(s - jnp.max(s, axis=1, keepdims=True))
            p = (s / jnp.sum(s, axis=1, keepdims=True)).astype(BF16)
            nb = 512 - t * 256
            o = dot(p[:, :nb], vp_ref[before, cols]) + dot(p[:, nb : nb + 512], v_ref[:, cols])
            o += dot(p[:, nb + 512 :], vn_ref[after, cols])
            out_ref[top, cols] = (o + learned_ref[top, cols]).astype(BF16)


def attend(*args):
    vmem = pl.BlockSpec(memory_space=pltpu.VMEM)
    return pl.pallas_call(
        attend_kernel,
        out_shape=jax.ShapeDtypeStruct((512, 1024), BF16),
        in_specs=[vmem] * 8,
        out_specs=vmem,
        compiler_params=pltpu.CompilerParams(vmem_limit_bytes=48 * 1024 * 1024),
        cost_estimate=pl.CostEstimate(flops=3_000_000_000, bytes_accessed=10_000_000, transcendentals=1_300_000),
        name="attend",
    )(*args)


def neighbours(value):
    up = [(i, i + 1) for i in range(63)]
    down = [(i + 1, i) for i in range(63)]
    return lax.ppermute(value, CTX, up), lax.ppermute(value, CTX, down)


def per_device(queries, keys, values, w_gate, w_up, w_out):
    spread = lambda value: lax.all_to_all(value, "head", split_axis=1, concat_axis=0, tiled=True)
    k, v, q = spread(keys), spread(values), spread(queries)
    kp, kn = neighbours(k)
    vp, vn = neighbours(v)
    learned = fast_weight(q, k, v, w_gate, w_up, w_out)
    mixed = attend(q, kp, k, kn, vp, v, vn, learned)
    return lax.all_to_all(mixed, "head", split_axis=0, concat_axis=1, tiled=True)


def solution(mesh):
    split = Mesh(mesh.devices.reshape(4, 4, 4, 4), ("head", Y, Z, X))
    rows_spec, heads_spec = P(CTX_HEAD, None), P("head", None, None)
    return jax.shard_map(
        per_device,
        mesh=split,
        in_specs=(rows_spec,) * 3 + (heads_spec,) * 3,
        out_specs=rows_spec,
        check_vma=False,
    )
```

time: 801 us -> 248 us (0.31)
  the two profiles are of different devices: /device:TPU:1 before, /device:TPU:32 now
where the time goes in v1:
time: 248 us
  Pallas kernels  113 us (46%)
  waiting for transfers between devices  64.2 us (26%)
  blocking collectives  35.8 us (14%)
  starting transfers between devices  26.4 us (11%)
  local copies, waits for them, and re-layouts  8.03 us (3%)
    pallas_call x1, Pallas kernels, fast_weight(): pl.pallas_call(fast_kernel, out_shape=jax.ShapeDtypeStruct((512, 1024), F...  105 us
    all_to_all x3, waiting for transfers between devices, per_device(): lax.all_to_all(value, 'head', split_axis=1, concat_axis=0, tiled=True)  64.2 us
    all_to_all x1, blocking collectives, per_device(): lax.all_to_all(mixed, 'head', split_axis=0, concat_axis=1, tiled=True)  35.8 us
    all_to_all x3, starting transfers between devices, per_device(): lax.all_to_all(value, 'head', split_axis=1, concat_axis=0, tiled=True)  14.6 us
    ppermute x4, starting transfers between devices, neighbours(): return (lax.ppermute(value, CTX, up), lax.ppermute(value, CTX, down))  11.8 us
    pallas_call x1, Pallas kernels, attend(): pl.pallas_call(attend_kernel, out_shape=jax.ShapeDtypeStruct((512, 1024),...  8.01 us
  transfers between devices with their start and end apart: 7, of which 3 were waited for; matrix products, arithmetic and copies ran while one was open for 1% of the time, Pallas kernels for 43%

profile of v1, /device:TPU:32, one launch (start us, length us, event | category | flops | bytes accessed | tf_op | source)
XLA Modules:
  0.0 247.9 jit_solution(9792105649488964443)
XLA Ops:
  0.0 0.0 copy-start.3
  0.0 2.4 copy.19
  2.4 7.6 %all-to-all-start.1 = ((bf16[128,4,1024]{2,0,1:T(8,128)(2,1)}), bf16[128,4,1024]{2,0,1:T(8,128)(2,1)S(1)}, u32[]{:S(2)}, u32[]{:S(2)}) async-start(bf16[128,4,1024]{2,0,1:T(8,128)(2,1)} %bitcast.23), calls=%async_computation.1 | async-start | bytes 2097152 | tf_op jit(solution)/shard_map/all_to_all | solution.py:296
  9.9 0.0 copy-done.3
  9.9 0.0 copy-start.4
  9.9 1.1 copy.18
  11.0 28.5 %all-to-all-done.1 = bf16[128,4,1024]{2,0,1:T(8,128)(2,1)S(1)} async-done(((bf16[128,4,1024]{2,0,1:T(8,128)(2,1)}), bf16[128,4,1024]{2,0,1:T(8,128)(2,1)S(1)}, u32[]{:S(2)}, u32[]{:S(2)}) %all-to-all-start.1) | async-done | bytes 1048608 | tf_op jit(solution)/shard_map/all_to_all | solution.py:296
  39.5 3.5 %all-to-all-start.2 = ((bf16[128,4,1024]{2,0,1:T(8,128)(2,1)}), bf16[128,4,1024]{2,0,1:T(8,128)(2,1)S(1)}, u32[]{:S(2)}, u32[]{:S(2)}) async-start(bf16[128,4,1024]{2,0,1:T(8,128)(2,1)} %bitcast.22), calls=%async_computation.2 | async-start | bytes 2097152 | tf_op jit(solution)/shard_map/all_to_all | solution.py:296
  43.0 0.0 copy-done.4
  43.0 1.1 copy.20
  44.1 28.6 %all-to-all-done.2 = bf16[128,4,1024]{2,0,1:T(8,128)(2,1)S(1)} async-done(((bf16[128,4,1024]{2,0,1:T(8,128)(2,1)}), bf16[128,4,1024]{2,0,1:T(8,128)(2,1)S(1)}, u32[]{:S(2)}, u32[]{:S(2)}) %all-to-all-start.2) | async-done | bytes 1048608 | tf_op jit(solution)/shard_map/all_to_all | solution.py:296
  72.7 0.0 copy-start
  72.7 3.5 %all-to-all-start = ((bf16[128,4,1024]{2,0,1:T(8,128)(2,1)}), bf16[128,4,1024]{2,0,1:T(8,128)(2,1)S(1)}, u32[]{:S(2)}, u32[]{:S(2)}) async-start(bf16[128,4,1024]{2,0,1:T(8,128)(2,1)} %bitcast.36), calls=%async_computation | async-start | bytes 2097152 | tf_op jit(solution)/shard_map/all_to_all | solution.py:296
  76.2 1.9 collective-permute-start.3
  78.1 3.9 %collective-permute-start.2 = (bf16[512,1024]{1,0:T(8,128)(2,1)S(1)}, bf16[512,1024]{1,0:T(8,128)(2,1)}, u32[]{:S(2)}, u32[]{:S(2)}) collective-permute-start(bf16[512,1024]{1,0:T(8,128)(2,1)S(1)} %bitcast.30), channel_id=1, source_target_pairs={{0,1},{1,2},{2,3},{3,4},{4,5},{5,6},{6,7},{7,8},{8,9},{9,10},{10,1... | collective-permute-start | bytes 3145736 | tf_op jit(solution)/shard_map/ppermute | solution.py:292
  82.0 4.0 %collective-permute-start.1 = (bf16[512,1024]{1,0:T(8,128)(2,1)S(1)}, bf16[512,1024]{1,0:T(8,128)(2,1)}, u32[]{:S(2)}, u32[]{:S(2)}) collective-permute-start(bf16[512,1024]{1,0:T(8,128)(2,1)S(1)} %bitcast.25), channel_id=1, source_target_pairs={{1,0},{2,1},{3,2},{4,3},{5,4},{6,5},{7,6},{8,7},{9,8},{10,9},{11,1... | collective-permute-start | bytes 3145736 | tf_op jit(solution)/shard_map/ppermute | solution.py:292
  86.1 1.9 collective-permute-start
  88.0 7.1 %all-to-all-done = bf16[128,4,1024]{2,0,1:T(8,128)(2,1)S(1)} async-done(((bf16[128,4,1024]{2,0,1:T(8,128)(2,1)}), bf16[128,4,1024]{2,0,1:T(8,128)(2,1)S(1)}, u32[]{:S(2)}, u32[]{:S(2)}) %all-to-all-start) | async-done | bytes 1048608 | tf_op jit(solution)/shard_map/all_to_all | solution.py:296
  95.1 0.0 copy-start.1
  95.1 1.2 copy-done.1
  96.4 0.0 copy-start.2
  96.4 1.2 copy-done.2
  97.6 105.4 %fast_weight.1.learned_ref = f32[512,1024]{1,0:T(8,128)} custom-call(bf16[512,1024]{1,0:T(8,128)(2,1)S(1)} %bitcast.33, bf16[512,1024]{1,0:T(8,128)(2,1)S(1)} %bitcast.27, bf16[512,1024]{1,0:T(8,128)(2,1)S(1)} %bitcast.31, bf16[2,512,512]{2,1,0:T(8,128)(2,1)S(1)} %copy-done.1, bf16[2,512,512]{2,1,0:T(8,128)(2,1)S(1)} %copy-done.2, bf16[2,512,512]{2,1,0:T(8,128)(2,1)} %wo_ref.1), custom_call_target="tpu_custom_call" | custom-call | flops 40000000000 | bytes 10000000 | tf_op jit(solution)/shard_map/fast_weight/pallas_call | solution.py:219
  203.0 0.0 copy-done
  203.0 0.0 collective-permute-done.3.vn_ref
  203.0 0.0 collective-permute-done.2.vp_ref
  203.0 0.0 collective-permute-done.1.kn_ref
  203.0 0.0 collective-permute-done.kp_ref
  203.1 8.0 %attend.1 = bf16[512,1024]{1,0:T(8,128)(2,1)S(1)} custom-call(bf16[512,1024]{1,0:T(8,128)(2,1)S(1)} %bitcast.34, bf16[512,1024]{1,0:T(8,128)(2,1)} %collective-permute-done.kp_ref, bf16[512,1024]{1,0:T(8,128)(2,1)S(1)} %bitcast.28, bf16[512,1024]{1,0:T(8,128)(2,1)} %collective-permute-done.1.kn_ref, bf16[512,1024]{1,0:T(8,128)(2,1)} %collective-permute-done.2.vp_ref, ...), custom_call_target="tpu_custom_call" | custom-call | flops 3000000000 | bytes 10000000 | tf_op jit(solution)/shard_map/attend/pallas_call | solution.py:278
  211.1 35.8 %all_to_all.76 = bf16[4,128,1024]{2,1,0:T(8,128)(2,1)S(1)} all-to-all(bf16[4,128,1024]{2,1,0:T(8,128)(2,1)S(1)} %bitcast.35), channel_id=1, replica_groups=mesh['head'=4,'ctx_0'=4,'ctx_1'=4,'ctx_2'=4] {'head'}, dimensions={0} | all-to-all | bytes 2097152 | tf_op jit(solution)/shard_map/all_to_all | solution.py:302
  246.9 1.1 copy.14
Async XLA Ops:
  0.0 9.9 %copy-start.3 = (bf16[128,4096]{1,0:T(8,128)(2,1)S(1)}, bf16[128,4096]{1,0:T(8,128)(2,1)}, u32[]{:S(2)}) copy-start(bf16[128,4096]{1,0:T(8,128)(2,1)} %param.8) | copy-start | bytes 3145732
  2.4 37.1 %all-to-all-start.1 = ((bf16[128,4,1024]{2,0,1:T(8,128)(2,1)}), bf16[128,4,1024]{2,0,1:T(8,128)(2,1)S(1)}, u32[]{:S(2)}, u32[]{:S(2)}) async-start(bf16[128,4,1024]{2,0,1:T(8,128)(2,1)} %bitcast.23), calls=%async_computation.1 | async-start | bytes 2097152 | tf_op jit(solution)/shard_map/all_to_all | solution.py:296
  9.9 33.1 %copy-start.4 = (bf16[128,4096]{1,0:T(8,128)(2,1)S(1)}, bf16[128,4096]{1,0:T(8,128)(2,1)}, u32[]{:S(2)}) copy-start(bf16[128,4096]{1,0:T(8,128)(2,1)} %param.6) | copy-start | bytes 3145732
  39.5 33.2 %all-to-all-start.2 = ((bf16[128,4,1024]{2,0,1:T(8,128)(2,1)}), bf16[128,4,1024]{2,0,1:T(8,128)(2,1)S(1)}, u32[]{:S(2)}, u32[]{:S(2)}) async-start(bf16[128,4,1024]{2,0,1:T(8,128)(2,1)} %bitcast.22), calls=%async_computation.2 | async-start | bytes 2097152 | tf_op jit(solution)/shard_map/all_to_all | solution.py:296
  72.7 130.4 %copy-start = (bf16[128,4,1024]{2,0,1:T(8,128)(2,1)}, bf16[128,4,1024]{2,0,1:T(8,128)(2,1)S(1)}, u32[]{:S(2)}) copy-start(bf16[128,4,1024]{2,0,1:T(8,128)(2,1)S(1)} %all-to-all-done.2) | copy-start | bytes 3145732
  72.7 22.5 %all-to-all-start = ((bf16[128,4,1024]{2,0,1:T(8,128)(2,1)}), bf16[128,4,1024]{2,0,1:T(8,128)(2,1)S(1)}, u32[]{:S(2)}, u32[]{:S(2)}) async-start(bf16[128,4,1024]{2,0,1:T(8,128)(2,1)} %bitcast.36), calls=%async_computation | async-start | bytes 2097152 | tf_op jit(solution)/shard_map/all_to_all | solution.py:296
  76.2 126.8 %collective-permute-start.3 = (bf16[512,1024]{1,0:T(8,128)(2,1)S(1)}, bf16[512,1024]{1,0:T(8,128)(2,1)}, u32[]{:S(2)}, u32[]{:S(2)}) collective-permute-start(bf16[512,1024]{1,0:T(8,128)(2,1)S(1)} %bitcast.29), channel_id=1, source_target_pairs={{1,0},{2,1},{3,2},{4,3},{5,4},{6,5},{7,6},{8,7},{9,8},{10,9},{11,1... | collective-permute-start | bytes 3145736 | tf_op jit(solution)/shard_map/ppermute | solution.py:292
  78.1 124.9 %collective-permute-start.2 = (bf16[512,1024]{1,0:T(8,128)(2,1)S(1)}, bf16[512,1024]{1,0:T(8,128)(2,1)}, u32[]{:S(2)}, u32[]{:S(2)}) collective-permute-start(bf16[512,1024]{1,0:T(8,128)(2,1)S(1)} %bitcast.30), channel_id=1, source_target_pairs={{0,1},{1,2},{2,3},{3,4},{4,5},{5,6},{6,7},{7,8},{8,9},{9,10},{10,1... | collective-permute-start | bytes 3145736 | tf_op jit(solution)/shard_map/ppermute | solution.py:292
  82.0 121.0 %collective-permute-start.1 = (bf16[512,1024]{1,0:T(8,128)(2,1)S(1)}, bf16[512,1024]{1,0:T(8,128)(2,1)}, u32[]{:S(2)}, u32[]{:S(2)}) collective-permute-start(bf16[512,1024]{1,0:T(8,128)(2,1)S(1)} %bitcast.25), channel_id=1, source_target_pairs={{1,0},{2,1},{3,2},{4,3},{5,4},{6,5},{7,6},{8,7},{9,8},{10,9},{11,1... | collective-permute-start | bytes 3145736 | tf_op jit(solution)/shard_map/ppermute | solution.py:292
  86.1 117.0 %collective-permute-start = (bf16[512,1024]{1,0:T(8,128)(2,1)S(1)}, bf16[512,1024]{1,0:T(8,128)(2,1)}, u32[]{:S(2)}, u32[]{:S(2)}) collective-permute-start(bf16[512,1024]{1,0:T(8,128)(2,1)S(1)} %bitcast.26), channel_id=1, source_target_pairs={{0,1},{1,2},{2,3},{3,4},{4,5},{5,6},{6,7},{7,8},{8,9},{9,10},{10,1... | collective-permute-start | bytes 3145736 | tf_op jit(solution)/shard_map/ppermute | solution.py:292
  95.1 1.2 copy-start.1
  96.4 1.2 copy-start.2

commit v2 on v1

v2 whole, which is shorter than its diff:
```python
import jax
import jax.numpy as jnp
from jax import lax
from jax.experimental import pallas as pl
from jax.experimental.pallas import tpu as pltpu
from jax.sharding import Mesh
from jax.sharding import PartitionSpec as P

HD = 512
WIN = 512
Y, Z, X = "ctx_0", "ctx_1", "ctx_2"
CTX = (Y, Z, X)
CTX_HEAD = CTX + ("head",)
MESH = pl.DeviceIdType.MESH
STEP = 0.02
EPS = 1e-06
F32, BF16 = jnp.float32, jnp.bfloat16


def dot(a, b, dims=((1,), (0,))):
    return lax.dot_general(a, b, (dims, ((), ())), preferred_element_type=F32)


class Copies:
    def __init__(self, send_sem, recv_sem):
        self.send_sem, self.recv_sem, self.count, self.all = send_sem, recv_sem, 0, []

    def make(self, src, dst, device):
        copy = pltpu.make_async_remote_copy(
            src_ref=src,
            dst_ref=dst,
            send_sem=self.send_sem.at[self.count],
            recv_sem=self.recv_sem.at[self.count],
            device_id=device,
            device_id_type=MESH,
        )
        self.count += 1
        self.all.append(copy)
        return copy

    def start(self, src, dst, device):
        copy = self.make(src, dst, device)
        copy.start()
        return copy


def ring(axis):
    me = lax.axis_index(axis)
    return me, lax.rem(me + 1, 4), lax.rem(me + 3, 4), lax.rem(me + 2, 4)


def rows(base, index, size, part=0, parts=1):
    step = size // parts
    return pl.ds(pl.multiple_of(base + index * size + part * step, 16), step)


def add_into(buf, at, other):
    buf[:, at, :] = (buf[:, at, :].astype(F32) + other.astype(F32)).astype(buf.dtype)


class RingReduce:
    def __init__(self, copies, axis, buf, c, opp, side):
        self.copies, self.axis, self.buf, self.c, self.opp, self.side = copies, axis, buf, c, opp, side
        me, right, left, far = ring(axis)
        half = c // 2
        r, l = {axis: right}, {axis: left}
        self.far_r = copies.start(buf.at[:, rows(0, far, c, 0, 2), :], opp.at[0], r)
        self.far_l = copies.start(buf.at[:, rows(0, far, c, 1, 2), :], opp.at[1], l)
        self.near_r = copies.start(buf.at[:, rows(0, right, c, 1, 2), :], side.at[0, :, pl.ds(half, half), :], r)
        self.near_l = copies.start(buf.at[:, rows(0, left, c, 0, 2), :], side.at[1, :, pl.ds(0, half), :], l)

    def middle(self):
        me, right, left, far = ring(self.axis)
        c, buf, half = self.c, self.buf, self.c // 2
        self.far_r.wait_recv()
        at = rows(0, right, c, 0, 2)
        add_into(buf, at, self.opp[0])
        self.last_r = self.copies.start(buf.at[:, at, :], self.side.at[0, :, pl.ds(0, half), :], {self.axis: right})
        self.far_l.wait_recv()
        at = rows(0, left, c, 1, 2)
        add_into(buf, at, self.opp[1])
        self.last_l = self.copies.start(buf.at[:, at, :], self.side.at[1, :, pl.ds(half, half), :], {self.axis: left})

    def end(self, out):
        me = lax.axis_index(self.axis)
        for copy in (self.near_r, self.near_l, self.last_r, self.last_l):
            copy.wait_recv()
        own = self.buf[:, rows(0, me, self.c), :].astype(F32)
        out[...] = own + self.side[0].astype(F32) + self.side[1].astype(F32)


class LineReduce:
    def __init__(self, copies, axis, buf, c, slots):
        me = lax.axis_index(axis)
        self.axis, self.buf, self.c, self.slots, self.sent = axis, buf, c, slots, []
        for d in (1, 2, 3):
            peer = lax.rem(me + d, 4)
            self.sent.append(copies.start(buf.at[:, rows(0, peer, c), :], slots.at[d - 1], {axis: peer}))

    def end(self):
        total = self.buf[:, rows(0, lax.axis_index(self.axis), self.c), :]
        for d in range(3):
            self.sent[d].wait_recv()
            total += self.slots[d]
        return total


class LineGather:
    def __init__(self, copies, axis, buf, base, c):
        me = lax.axis_index(axis)
        at = buf.at[:, rows(base, me, c), :]
        self.sent = [copies.start(at, at, {axis: lax.rem(me + d, 4)}) for d in (1, 2, 3)]

    def end(self):
        for copy in self.sent:
            copy.wait_recv()


class RingGather:
    def __init__(self, copies, axis, buf, base, c):
        self.copies, self.axis, self.buf, self.base, self.c = copies, axis, buf, base, c
        me, right, left, far = ring(axis)
        low, high = (buf.at[:, rows(base, me, c, part, 2), :] for part in (0, 1))
        self.low_r = copies.start(low, low, {axis: right})
        self.high_l = copies.start(high, high, {axis: left})
        self.high_r = copies.start(high, high, {axis: right})
        self.low_l = copies.start(low, low, {axis: left})

    def middle(self):
        me, right, left, far = ring(self.axis)
        self.low_r.wait_recv()
        at = self.buf.at[:, rows(self.base, left, self.c, 0, 2), :]
        self.far_r = self.copies.start(at, at, {self.axis: right})
        self.high_l.wait_recv()
        at = self.buf.at[:, rows(self.base, right, self.c, 1, 2), :]
        self.far_l = self.copies.start(at, at, {self.axis: left})

    def end(self):
        for copy in (self.high_r, self.low_l, self.far_r, self.far_l):
            copy.wait_recv()


class Group:
    def __init__(self, copies, g, bufs):
        self.copies, self.g = copies, g
        self.first, self.second = ((X, Y), (Y, X))[g % 2]
        self.b = {name: ref.at[g] for name, ref in bufs.items()}
        self.base = lax.axis_index(self.first) * 256
        self.inner = self.base + lax.axis_index(self.second) * 64

    def start(self):
        b = self.b
        self.now = RingReduce(self.copies, self.first, b["grad"], 256, b["opp1"], b["side1"])

    def middle(self):
        self.now.middle()

    def start2(self):
        b = self.b
        self.now.end(b["part2"])
        self.now = RingReduce(self.copies, self.second, b["part2"], 64, b["opp2"], b["side2"])

    def start3(self):
        b = self.b
        self.now.end(b["part3"])
        self.now = LineReduce(self.copies, Z, b["part3"], 16, b["slots"])

    def gather3(self):
        b = self.b
        b["total"][:, rows(self.inner, lax.axis_index(Z), 16), :] = self.now.end().astype(BF16)
        self.now = LineGather(self.copies, Z, b["total"], self.inner, 16)

    def gather2(self):
        self.now.end()
        self.now = RingGather(self.copies, self.second, self.b["total"], self.base, 64)

    def gather1(self):
        self.now.end()
        self.now = RingGather(self.copies, self.first, self.b["total"], 0, 256)

    def end(self):
        self.now.end()


def gradients(k, v, wg, wu, wo, grad, h):
    a, b = dot(k, wg), dot(k, wu)
    back = -dot(v, wo, ((1,), (1,)))
    sig = jax.nn.sigmoid(a)
    act = a * sig
    hidden = (act * b).astype(BF16)
    da = (back * b * (sig * (1.0 + a * (1.0 - sig)))).astype(BF16)
    db = (back * act).astype(BF16)
    pairs = ((k, da), (k, db), (hidden, v))
    for m, (left, right) in enumerate(pairs):
        g = dot(left, right, ((0,), (0,)))
        g = -g if m == 2 else g
        for part in range(4):
            at = pl.ds((part % 2) * HD, HD)
            grad[2 * h + part // 2, m, at, :] = g[:, part * 128 : part * 128 + 128].astype(BF16)


def update(total, weights, fresh, h):
    for m, w_ref in enumerate(weights):
        squares = 0.0
        for color in range(2):
            g = total[2 * h + color, m].astype(F32)
            squares += jnp.sum(g * g)
        scale = STEP * lax.rsqrt(squares / (HD * HD) + EPS)
        for part in range(4):
            cols = pl.ds(part * 128, 128)
            g = total[2 * h + part // 2, m, pl.ds((part % 2) * HD, HD), :].astype(F32)
            fresh[m, :, cols] = (w_ref[h, :, cols].astype(F32) - scale * g).astype(BF16)


def attention(q_ref, before, own, after, out, has_before, has_after):
    r = lax.broadcasted_iota(jnp.int32, (256, 256), 0)
    c = lax.broadcasted_iota(jnp.int32, (256, 256), 1)
    for t in range(2):
        top = pl.ds(t * 256, 256)
        q = q_ref[top, :]
        nb = 512 - t * 256
        late, early = pl.ds(t * 256, nb), pl.ds(0, 256 + t * 256)
        sb = dot(q, before[0, late, :], ((1,), (1,))) * HD**-0.5
        so = dot(q, own[0], ((1,), (1,))) * HD**-0.5
        sa = dot(q, after[0, early, :], ((1,), (1,))) * HD**-0.5
        pieces = [jnp.where((c >= r) & has_before, sb[:, :256], -1e30)]
        if t == 0:
            pieces += [jnp.where(has_before, sb[:, 256:], -1e30), so]
        else:
            pieces += [so, jnp.where(has_after, sa[:, :256], -1e30)]
        pieces.append(jnp.where((c <= r) & has_after, sa[:, t * 256 :], -1e30))
        s = jnp.concatenate(pieces, axis=1)
        s = jnp.exp(s - jnp.max(s, axis=1, keepdims=True))
        p = (s / jnp.sum(s, axis=1, keepdims=True)).astype(BF16)
        o = dot(p[:, :nb], before[1, late, :]) + dot(p[:, nb : nb + 512], own[1])
        out[top, :] = o + dot(p[:, nb + 512 :], after[1, early, :])


def shifted(delta):
    block = (lax.axis_index(Y) * 4 + lax.axis_index(Z)) * 4 + lax.axis_index(X)
    to = lax.rem(block + delta + 64, 64)
    return {Y: to // 16, Z: lax.rem(to // 4, 4), X: lax.rem(to, 4)}


def kernel(
    q_in, k_in, v_in, wg_in, wu_in, wo_in, out_ref,
    wg, wu, wo, q_all, kv, before, after, attended, mixed, fresh,
    grad, opp1, side1, part2, opp2, side2, part3, slots, total, send_sem, recv_sem, local_sem,
):
    g = lax.axis_index("head")
    hi, core = g // 2, lax.rem(g, 2)
    heads = ((1 - hi) * 2 + core, (1 - hi) * 2 + 1 - core, hi * 2 + 1 - core)
    barrier = pltpu.get_barrier_semaphore()
    partners = [{"head": p} for p in heads] + [shifted(1), shifted(-1)]
    for axis, offsets in ((X, (1, 3)), (Y, (1, 3)), (Z, (1, 2, 3))):
        partners += [{axis: lax.rem(lax.axis_index(axis) + d, 4)} for d in offsets]
    for p in partners:
        pl.semaphore_signal(barrier, inc=1, device_id=p, device_id_type=MESH)

    def cols(p, h):
        return pl.ds(pl.multiple_of(p * 1024 + h * HD, HD), HD)

    def place(ref, p):
        return ref.at[pl.ds(pl.multiple_of(p * 128, 128), 128), :]

    def half_rows(p):
        return pl.ds(pl.multiple_of(p * 256, 256), 256)

    local = []

    def stay(src, dst):
        copy = pltpu.make_async_copy(src, dst, local_sem.at[len(local)])
        copy.start()
        local.append(copy)

    for h in range(2):
        for i, ref in enumerate((k_in, v_in)):
            stay(ref.at[:, cols(g, h)], place(kv.at[i, h], g))
        stay(q_in.at[:, cols(g, h)], place(q_all.at[h], g))
    for src, dst in ((wg_in, wg), (wu_in, wu), (wo_in, wo)):
        stay(src, dst)

    copies = Copies(send_sem, recv_sem)
    pl.semaphore_wait(barrier, len(partners))
    sent = {}
    for h in range(2):
        for j, p in enumerate(heads):
            for i, ref in enumerate((k_in, v_in)):
                sent[h, j, i] = copies.start(ref.at[:, cols(p, h)], place(kv.at[i, h], g), {"head": p})
    for h in range(2):
        for j, p in enumerate(heads):
            sent[h, j, 2] = copies.start(q_in.at[:, cols(p, h)], place(q_all.at[h], g), {"head": p})

    def halo(src_index, at):
        found = []
        for dst, delta in ((before, 1), (after, -1)):
            found.append(copies.start(kv.at[src_index + (at, slice(None))], dst.at[src_index + (at, slice(None))], shifted(delta)))
        return found

    for copy in local:
        copy.wait()
    for h in range(2):
        for i in range(2):
            sent[h, 2, i].wait_recv()
    every = slice(None)
    halos = halo((every, every), half_rows(hi))

    bufs = dict(
        grad=grad, opp1=opp1, side1=side1, part2=part2, opp2=opp2, side2=side2, part3=part3, slots=slots, total=total
    )
    groups = [Group(copies, n, bufs) for n in range(4)]
    weights = (wg, wu, wo)

    def both(h, step):
        for group in groups[2 * h : 2 * h + 2]:
            getattr(group, step)()

    def head_in(h):
        for j in range(2):
            for i in range(2):
                sent[h, j, i].wait_recv()
        gradients(kv[0, h], kv[1, h], wg[h], wu[h], wo[h], grad, h)
        both(h, "start")

    has_before = sum(lax.axis_index(axis) for axis in CTX) > 0
    has_after = sum(lax.axis_index(axis) for axis in CTX) < 9

    def attend(h):
        attention(q_all.at[h], before.at[:, h], kv.at[:, h], after.at[:, h], attended.at[h], has_before, has_after)

    outs = {}

    def learn(h):
        update(total, weights, fresh, h)
        q = q_all[h]
        gate = dot(q, fresh[0])
        hid = (gate * jax.nn.sigmoid(gate) * dot(q, fresh[1])).astype(BF16)
        mixed[h] = (attended[h] + dot(hid, fresh[2])).astype(BF16)
        for j, p in enumerate(heads):
            outs[h, j] = copies.start(place(mixed.at[h], p), out_ref.at[:, cols(g, h)], {"head": p})
        out_ref[:, cols(g, h)] = mixed[h, pl.ds(pl.multiple_of(g * 128, 128), 128), :]

    head_in(0)
    both(0, "middle")
    both(0, "start2")
    both(0, "middle")
    halos += halo((every, 0), half_rows(1 - hi))
    both(0, "start3")
    head_in(1)
    both(0, "gather3")
    both(1, "middle")
    both(0, "gather2")
    both(1, "start2")
    both(0, "middle")
    both(1, "middle")
    halos += halo((every, 1), half_rows(1 - hi))
    both(0, "gather1")
    both(1, "start3")
    both(0, "middle")
    both(1, "gather3")
    both(1, "gather2")
    both(1, "middle")
    for copy in halos[:4]:
        copy.wait_recv()
    for h in range(2):
        for j in range(3):
            sent[h, j, 2].wait_recv()
    both(1, "gather1")
    attend(0)
    both(0, "end")
    both(1, "middle")
    learn(0)
    for copy in halos[4:]:
        copy.wait_recv()
    attend(1)
    both(1, "end")
    learn(1)
    for copy in outs.values():
        copy.wait_recv()
    for copy in copies.all:
        copy.wait_send()


def per_device(queries, keys, values, w_gate, w_up, w_out):
    anywhere = pl.BlockSpec(memory_space=pl.ANY)
    n_copies = 150
    wide, matrices = (2, HD, HD), (3, HD, HD)
    return pl.pallas_call(
        kernel,
        out_shape=jax.ShapeDtypeStruct((128, 4096), BF16),
        in_specs=[anywhere] * 6,
        out_specs=pl.BlockSpec(memory_space=pltpu.VMEM),
        scratch_shapes=[
            pltpu.VMEM(wide, BF16),
            pltpu.VMEM(wide, BF16),
            pltpu.VMEM(wide, BF16),
            pltpu.VMEM(wide, BF16),
            pltpu.VMEM((2,) + wide, BF16),
            pltpu.VMEM((2,) + wide, BF16),
            pltpu.VMEM((2,) + wide, BF16),
            pltpu.VMEM(wide, F32),
            pltpu.VMEM(wide, BF16),
            pltpu.VMEM(matrices, BF16),
            pltpu.VMEM((4, 3, 1024, 128), BF16),
            pltpu.VMEM((4, 2, 3, 128, 128), BF16),
            pltpu.VMEM((4, 2, 3, 256, 128), BF16),
            pltpu.VMEM((4, 3, 256, 128), F32),
            pltpu.VMEM((4, 2, 3, 32, 128), F32),
            pltpu.VMEM((4, 2, 3, 64, 128), F32),
            pltpu.VMEM((4, 3, 64, 128), F32),
            pltpu.VMEM((4, 3, 3, 16, 128), F32),
            pltpu.VMEM((4, 3, 1024, 128), BF16),
            pltpu.SemaphoreType.DMA((n_copies,)),
            pltpu.SemaphoreType.DMA((n_copies,)),
            pltpu.SemaphoreType.DMA((9,)),
        ],
        compiler_params=pltpu.CompilerParams(
            collective_id=0, has_side_effects=True, vmem_limit_bytes=56 * 1024 * 1024
        ),
        name="layer",
    )(queries, keys, values, w_gate, w_up, w_out)


def solution(mesh):
    split = Mesh(mesh.devices.reshape(4, 4, 4, 4), ("head", Y, Z, X))
    rows_spec, heads_spec = P(CTX_HEAD, None), P("head", None, None)
    return jax.shard_map(
        per_device,
        mesh=split,
        in_specs=(rows_spec,) * 3 + (heads_spec,) * 3,
        out_specs=rows_spec,
        check_vma=False,
    )
```

time: 248 us -> 189 us (0.76)
  the two profiles are of different devices: /device:TPU:32 before, /device:TPU:1 now
where the time goes in v2:
time: 189 us
  Pallas kernels  187 us (99%)
  local copies, waits for them, and re-layouts  2.29 us (1%)
    pallas_call x1, Pallas kernels, per_device(): pl.pallas_call(kernel, out_shape=jax.ShapeDtypeStruct((128, 4096), BF16),...  187 us

profile of v2, /device:TPU:1, one launch (start us, length us, event | category | flops | bytes accessed | tf_op | source)
XLA Modules:
  0.0 189.2 jit_solution(16959395616668412521)
XLA Ops:
  0.0 186.9 %layer.1 = bf16[128,4096]{1,0:T(8,128)(2,1)} custom-call(bf16[128,4096]{1,0:T(8,128)(2,1)} %q_in.1, bf16[128,4096]{1,0:T(8,128)(2,1)} %k_in.1, bf16[128,4096]{1,0:T(8,128)(2,1)} %v_in.1, bf16[2,512,512]{2,1,0:T(8,128)(2,1)} %wg_in.1, bf16[2,512,512]{2,1,0:T(8,128)(2,1)} %wu_in.1, bf16[2,512,512]{2,1,0:T(8,128)(2,1)} %wo_in.1), custom_call_target="tpu_custom_call" | custom-call | tf_op jit(solution)/shard_map/layer/pallas_call | solution.py:388
  186.9 2.3 %copy.8 = bf16[128,4096]{1,0:T(8,128)(2,1)} copy(bf16[128,4096]{1,0:T(8,128)(2,1)} %layer.1) | data formatting | bytes 2097152

commit v3 on v2

--- a/solution.py
+++ b/solution.py
@@ -35,11 +35,11 @@
             device_id_type=MESH,
         )
         self.count += 1
-        self.all.append(copy)
         return copy
 
     def start(self, src, dst, device):
         copy = self.make(src, dst, device)
+        self.all.append(copy)
         copy.start()
         return copy
 
@@ -236,35 +236,105 @@
         out[top, :] = o + dot(p[:, nb + 512 :], after[1, early, :])
 
 
-def shifted(delta):
-    block = (lax.axis_index(Y) * 4 + lax.axis_index(Z)) * 4 + lax.axis_index(X)
-    to = lax.rem(block + delta + 64, 64)
-    return {Y: to // 16, Z: lax.rem(to // 4, 4), X: lax.rem(to, 4)}
+def row(delta, x):
+    to = lax.rem(lax.axis_index(Y) * 4 + lax.axis_index(Z) + delta + 16, 16)
+    return {Y: to // 4, Z: lax.rem(to, 4), X: jnp.int32(x)}
+
+
+class Halo:
+    def __init__(self, copies, kv, dst, relay, delta, hi):
+        x = lax.axis_index(X)
+        self.source, self.last = (3, 0) if delta == 1 else (0, 3)
+        self.x, self.copies = x, copies
+        self.is_source, self.is_last = x == self.source, x == self.last
+        nearby = {X: lax.rem(x + delta + 4, 4)}
+        every = slice(None)
+        own = pl.ds(pl.multiple_of(hi * 256, 256), 256)
+        other = pl.ds(pl.multiple_of((1 - hi) * 256, 256), 256)
+        self.early = copies.make(kv.at[:, :, own, :], dst.at[:, :, own, :], nearby)
+        self.cross = [copies.make(kv.at[:, h, other, :], dst.at[:, h, other, :], nearby) for h in range(2)]
+        self.leg1, self.leg2 = {}, {}
+        for c in range(4):
+            piece = kv.at[c % 2, c // 2]
+            if c != self.source:
+                self.leg1[c] = copies.make(piece, relay, {X: jnp.int32(c)})
+                piece = relay
+            self.leg2[c] = copies.make(piece, dst.at[c % 2, c // 2], row(delta, self.last))
+
+    def send_early(self):
+        pl.when(jnp.logical_not(self.is_source))(self.early.start)
+
+    def send(self, h):
+        pl.when(jnp.logical_not(self.is_source))(self.cross[h].start)
+
+        @pl.when(self.is_source)
+        def _():
+            for c in (2 * h, 2 * h + 1):
+                (self.leg2 if c == self.source else self.leg1)[c].start()
+
+    def relay(self, h):
+        for c in (2 * h, 2 * h + 1):
+            if c != self.source:
+
+                @pl.when(self.x == c)
+                def _():
+                    self.leg1[c].wait_recv()
+                    self.leg2[c].start()
+
+    def receive(self, h):
+        @pl.when(self.is_last)
+        def _():
+            for c in (2 * h, 2 * h + 1):
+                self.leg2[c].wait_recv()
+
+        @pl.when(jnp.logical_not(self.is_last))
+        def _():
+            if h == 0:
+                self.early.wait_recv()
+            self.cross[h].wait_recv()
+
+    def finish(self):
+        @pl.when(jnp.logical_not(self.is_source))
+        def _():
+            self.early.wait_send()
+            for h in range(2):
+                self.cross[h].wait_send()
+
+        @pl.when(self.is_source)
+        def _():
+            for copy in self.leg1.values():
+                copy.wait_send()
+
+        for c in range(4):
+            pl.when(self.x == c)(self.leg2[c].wait_send)
 
 
 def kernel(
     q_in, k_in, v_in, wg_in, wu_in, wo_in, out_ref,
-    wg, wu, wo, q_all, kv, before, after, attended, mixed, fresh,
+    wg, wu, wo, q_all, kv, before, after, relays, attended, mixed, fresh,
     grad, opp1, side1, part2, opp2, side2, part3, slots, total, send_sem, recv_sem, local_sem,
 ):
     g = lax.axis_index("head")
     hi, core = g // 2, lax.rem(g, 2)
     heads = ((1 - hi) * 2 + core, (1 - hi) * 2 + 1 - core, hi * 2 + 1 - core)
     barrier = pltpu.get_barrier_semaphore()
-    partners = [{"head": p} for p in heads] + [shifted(1), shifted(-1)]
-    for axis, offsets in ((X, (1, 3)), (Y, (1, 3)), (Z, (1, 2, 3))):
+    partners = [{"head": p} for p in heads]
+    for axis, offsets in ((X, (1, 2, 3)), (Y, (1, 3)), (Z, (1, 2, 3))):
         partners += [{axis: lax.rem(lax.axis_index(axis) + d, 4)} for d in offsets]
     for p in partners:
         pl.semaphore_signal(barrier, inc=1, device_id=p, device_id_type=MESH)
+    for x, delta in ((0, -1), (3, 1)):
+
+        @pl.when(lax.axis_index(X) == x)
+        def _():
+            for c in range(4):
+                pl.semaphore_signal(barrier, inc=1, device_id=row(delta, c), device_id_type=MESH)
 
     def cols(p, h):
         return pl.ds(pl.multiple_of(p * 1024 + h * HD, HD), HD)
 
     def place(ref, p):
         return ref.at[pl.ds(pl.multiple_of(p * 128, 128), 128), :]
-
-    def half_rows(p):
-        return pl.ds(pl.multiple_of(p * 256, 256), 256)
 
     local = []
 
@@ -281,29 +351,29 @@
         stay(src, dst)
 
     copies = Copies(send_sem, recv_sem)
-    pl.semaphore_wait(barrier, len(partners))
+    pl.semaphore_wait(barrier, len(partners) + 2)
     sent = {}
     for h in range(2):
         for j, p in enumerate(heads):
             for i, ref in enumerate((k_in, v_in)):
                 sent[h, j, i] = copies.start(ref.at[:, cols(p, h)], place(kv.at[i, h], g), {"head": p})
-    for h in range(2):
+
+    def send_queries(h):
         for j, p in enumerate(heads):
             sent[h, j, 2] = copies.start(q_in.at[:, cols(p, h)], place(q_all.at[h], g), {"head": p})
 
-    def halo(src_index, at):
-        found = []
-        for dst, delta in ((before, 1), (after, -1)):
-            found.append(copies.start(kv.at[src_index + (at, slice(None))], dst.at[src_index + (at, slice(None))], shifted(delta)))
-        return found
+    halos = [Halo(copies, kv, dst, relays.at[j], delta, hi) for j, (dst, delta) in enumerate(((before, 1), (after, -1)))]
+
+    def halo(step, *args):
+        for h in halos:
+            getattr(h, step)(*args)
 
     for copy in local:
         copy.wait()
     for h in range(2):
         for i in range(2):
             sent[h, 2, i].wait_recv()
-    every = slice(None)
-    halos = halo((every, every), half_rows(hi))
+    halo("send_early")
 
     bufs = dict(
         grad=grad, opp1=opp1, side1=side1, part2=part2, opp2=opp2, side2=side2, part3=part3, slots=slots, total=total
@@ -326,6 +396,9 @@
     has_after = sum(lax.axis_index(axis) for axis in CTX) < 9
 
     def attend(h):
+        halo("receive", h)
+        for j in range(3):
+            sent[h, j, 2].wait_recv()
         attention(q_all.at[h], before.at[:, h], kv.at[:, h], after.at[:, h], attended.at[h], has_before, has_after)
 
     outs = {}
@@ -343,47 +416,45 @@
     head_in(0)
     both(0, "middle")
     both(0, "start2")
+    halo("send", 0)
     both(0, "middle")
-    halos += halo((every, 0), half_rows(1 - hi))
     both(0, "start3")
+    send_queries(0)
     head_in(1)
+    halo("relay", 0)
     both(0, "gather3")
     both(1, "middle")
+    send_queries(1)
     both(0, "gather2")
     both(1, "start2")
+    halo("send", 1)
     both(0, "middle")
     both(1, "middle")
-    halos += halo((every, 1), half_rows(1 - hi))
     both(0, "gather1")
     both(1, "start3")
+    halo("relay", 1)
     both(0, "middle")
     both(1, "gather3")
+    attend(0)
     both(1, "gather2")
+    both(0, "end")
+    learn(0)
     both(1, "middle")
-    for copy in halos[:4]:
-        copy.wait_recv()
-    for h in range(2):
-        for j in range(3):
-            sent[h, j, 2].wait_recv()
     both(1, "gather1")
-    attend(0)
-    both(0, "end")
+    attend(1)
     both(1, "middle")
-    learn(0)
-    for copy in halos[4:]:
-        copy.wait_recv()
-    attend(1)
     both(1, "end")
     learn(1)
     for copy in outs.values():
         copy.wait_recv()
     for copy in copies.all:
         copy.wait_send()
+    halo("finish")
 
 
 def per_device(queries, keys, values, w_gate, w_up, w_out):
     anywhere = pl.BlockSpec(memory_space=pl.ANY)
-    n_copies = 150
+    n_copies = 164
     wide, matrices = (2, HD, HD), (3, HD, HD)
     return pl.pallas_call(
         kernel,
@@ -398,6 +469,7 @@
             pltpu.VMEM((2,) + wide, BF16),
             pltpu.VMEM((2,) + wide, BF16),
             pltpu.VMEM((2,) + wide, BF16),
+            pltpu.VMEM(wide, BF16),
             pltpu.VMEM(wide, F32),
             pltpu.VMEM(wide, BF16),
             pltpu.VMEM(matrices, BF16),

time: 189 us -> 228 us (1.21)
  the two profiles are of different devices: /device:TPU:1 before, /device:TPU:225 now
where the time goes in v3:
time: 228 us
  Pallas kernels  226 us (99%)
  local copies, waits for them, and re-layouts  2.29 us (1%)
    pallas_call x1, Pallas kernels, per_device(): pl.pallas_call(kernel, out_shape=jax.ShapeDtypeStruct((128, 4096), BF16),...  226 us

profile of v3, /device:TPU:225, one launch (start us, length us, event | category | flops | bytes accessed | tf_op | source)
XLA Modules:
  0.0 228.4 jit_solution(18287443132611510476)
XLA Ops:
  0.0 226.1 %layer.1 = bf16[128,4096]{1,0:T(8,128)(2,1)} custom-call(bf16[128,4096]{1,0:T(8,128)(2,1)} %q_in.1, bf16[128,4096]{1,0:T(8,128)(2,1)} %k_in.1, bf16[128,4096]{1,0:T(8,128)(2,1)} %v_in.1, bf16[2,512,512]{2,1,0:T(8,128)(2,1)} %wg_in.1, bf16[2,512,512]{2,1,0:T(8,128)(2,1)} %wu_in.1, bf16[2,512,512]{2,1,0:T(8,128)(2,1)} %wo_in.1), custom_call_target="tpu_custom_call" | custom-call | tf_op jit(solution)/shard_map/layer/pallas_call | solution.py:459
  226.1 2.3 %copy.8 = bf16[128,4096]{1,0:T(8,128)(2,1)} copy(bf16[128,4096]{1,0:T(8,128)(2,1)} %layer.1) | data formatting | bytes 2097152

commit v4 on v3

--- a/solution.py
+++ b/solution.py
@@ -143,7 +143,7 @@
 class Group:
     def __init__(self, copies, g, bufs):
         self.copies, self.g = copies, g
-        self.first, self.second = ((X, Y), (Y, X))[g % 2]
+        self.first, self.second = (Y, X)
         self.b = {name: ref.at[g] for name, ref in bufs.items()}
         self.base = lax.axis_index(self.first) * 256
         self.inner = self.base + lax.axis_index(self.second) * 64
@@ -236,30 +236,31 @@
         out[top, :] = o + dot(p[:, nb + 512 :], after[1, early, :])
 
 
-def row(delta, x):
-    to = lax.rem(lax.axis_index(Y) * 4 + lax.axis_index(Z) + delta + 16, 16)
-    return {Y: to // 4, Z: lax.rem(to, 4), X: jnp.int32(x)}
-
-
 class Halo:
-    def __init__(self, copies, kv, dst, relay, delta, hi):
-        x = lax.axis_index(X)
+    def __init__(self, copies, kv, dst, relays, delta, hi):
+        x, y, z = (lax.axis_index(axis) for axis in (X, Y, Z))
         self.source, self.last = (3, 0) if delta == 1 else (0, 3)
-        self.x, self.copies = x, copies
+        self.x = x
         self.is_source, self.is_last = x == self.source, x == self.last
+        self.leaves_y, self.enters_y = z == self.source, z == self.last
+        ahead = lax.rem(z + delta + 4, 4)
+        onward = lax.select(self.enters_y, lax.rem(y + delta + 4, 4), y)
         nearby = {X: lax.rem(x + delta + 4, 4)}
         every = slice(None)
         own = pl.ds(pl.multiple_of(hi * 256, 256), 256)
         other = pl.ds(pl.multiple_of((1 - hi) * 256, 256), 256)
         self.early = copies.make(kv.at[:, :, own, :], dst.at[:, :, own, :], nearby)
         self.cross = [copies.make(kv.at[:, h, other, :], dst.at[:, h, other, :], nearby) for h in range(2)]
-        self.leg1, self.leg2 = {}, {}
+        self.leg1, self.leg2, self.leg3 = {}, {}, {}
         for c in range(4):
-            piece = kv.at[c % 2, c // 2]
+            piece, end = kv.at[c % 2, c // 2], dst.at[c % 2, c // 2]
             if c != self.source:
-                self.leg1[c] = copies.make(piece, relay, {X: jnp.int32(c)})
-                piece = relay
-            self.leg2[c] = copies.make(piece, dst.at[c % 2, c // 2], row(delta, self.last))
+                self.leg1[c] = copies.make(piece, relays.at[0], {X: jnp.int32(c)})
+                piece = relays.at[0]
+            self.leg2[c] = copies.make(piece, relays.at[1], {Z: ahead})
+            if c == self.last:
+                self.short = copies.make(piece, end, {Z: ahead})
+            self.leg3[c] = copies.make(relays.at[1], end, {Y: onward, X: jnp.int32(self.last)})
 
     def send_early(self):
         pl.when(jnp.logical_not(self.is_source))(self.early.start)
@@ -270,22 +271,47 @@
         @pl.when(self.is_source)
         def _():
             for c in (2 * h, 2 * h + 1):
-                (self.leg2 if c == self.source else self.leg1)[c].start()
+                if c != self.source:
+                    self.leg1[c].start()
+
+    def second(self, c, step):
+        if c == self.last:
+            pl.when((self.x == c) & self.leaves_y)(lambda: getattr(self.leg2[c], step)())
+            pl.when((self.x == c) & jnp.logical_not(self.leaves_y))(lambda: getattr(self.short, step)())
+        else:
+            pl.when(self.x == c)(lambda: getattr(self.leg2[c], step)())
+
+    def third(self, c):
+        return (self.x == c) & self.enters_y if c == self.last else self.x == c
 
     def relay(self, h):
         for c in (2 * h, 2 * h + 1):
             if c != self.source:
-
-                @pl.when(self.x == c)
-                def _():
-                    self.leg1[c].wait_recv()
-                    self.leg2[c].start()
+                pl.when(self.x == c)(self.leg1[c].wait_recv)
+            self.second(c, "start")
+
+    def forward(self, c, condition):
+        @pl.when((self.x == c) & condition)
+        def _():
+            self.leg2[c].wait_recv()
+            self.leg3[c].start()
+
+    def relay2(self, h):
+        for c in (2 * h, 2 * h + 1):
+            if c != self.last:
+                self.forward(c, jnp.logical_not(self.enters_y))
+
+    def relay2_y(self):
+        for c in range(4):
+            self.forward(c, self.enters_y)
 
     def receive(self, h):
-        @pl.when(self.is_last)
-        def _():
-            for c in (2 * h, 2 * h + 1):
-                self.leg2[c].wait_recv()
+        for c in (2 * h, 2 * h + 1):
+            if c == self.last:
+                pl.when(self.is_last & self.enters_y)(self.leg3[c].wait_recv)
+                pl.when(self.is_last & jnp.logical_not(self.enters_y))(self.short.wait_recv)
+            else:
+                pl.when(self.is_last)(self.leg3[c].wait_recv)
 
         @pl.when(jnp.logical_not(self.is_last))
         def _():
@@ -306,7 +332,8 @@
                 copy.wait_send()
 
         for c in range(4):
-            pl.when(self.x == c)(self.leg2[c].wait_send)
+            self.second(c, "wait_send")
+            pl.when(self.third(c))(self.leg3[c].wait_send)
 
 
 def kernel(
@@ -323,12 +350,13 @@
         partners += [{axis: lax.rem(lax.axis_index(axis) + d, 4)} for d in offsets]
     for p in partners:
         pl.semaphore_signal(barrier, inc=1, device_id=p, device_id_type=MESH)
-    for x, delta in ((0, -1), (3, 1)):
-
-        @pl.when(lax.axis_index(X) == x)
+    for corner, step in ((0, 3), (3, 1)):
+        above = {Y: lax.rem(lax.axis_index(Y) + step, 4)}
+
+        @pl.when(lax.axis_index(X) == corner)
         def _():
             for c in range(4):
-                pl.semaphore_signal(barrier, inc=1, device_id=row(delta, c), device_id_type=MESH)
+                pl.semaphore_signal(barrier, inc=1, device_id=above | {X: jnp.int32(c)}, device_id_type=MESH)
 
     def cols(p, h):
         return pl.ds(pl.multiple_of(p * 1024 + h * HD, HD), HD)
@@ -353,10 +381,14 @@
     copies = Copies(send_sem, recv_sem)
     pl.semaphore_wait(barrier, len(partners) + 2)
     sent = {}
-    for h in range(2):
-        for j, p in enumerate(heads):
+
+    def send_pairs(h, js):
+        for j in js:
             for i, ref in enumerate((k_in, v_in)):
-                sent[h, j, i] = copies.start(ref.at[:, cols(p, h)], place(kv.at[i, h], g), {"head": p})
+                sent[h, j, i] = copies.start(ref.at[:, cols(heads[j], h)], place(kv.at[i, h], g), {"head": heads[j]})
+
+    send_pairs(0, (0, 1, 2))
+    send_pairs(1, (2,))
 
     def send_queries(h):
         for j, p in enumerate(heads):
@@ -389,6 +421,12 @@
         for j in range(2):
             for i in range(2):
                 sent[h, j, i].wait_recv()
+        if h == 0:
+            send_pairs(1, (0, 1))
+            halo("send", 0)
+        else:
+            send_queries(0)
+            send_queries(1)
         gradients(kv[0, h], kv[1, h], wg[h], wu[h], wo[h], grad, h)
         both(h, "start")
 
@@ -415,34 +453,34 @@
 
     head_in(0)
     both(0, "middle")
+    head_in(1)
     both(0, "start2")
-    halo("send", 0)
+    both(1, "middle")
     both(0, "middle")
+    both(1, "start2")
     both(0, "start3")
-    send_queries(0)
-    head_in(1)
+    both(1, "middle")
+    both(1, "start3")
+    halo("send", 1)
+    both(0, "gather3")
+    both(1, "gather3")
+    both(0, "gather2")
+    both(1, "gather2")
     halo("relay", 0)
-    both(0, "gather3")
-    both(1, "middle")
-    send_queries(1)
-    both(0, "gather2")
-    both(1, "start2")
-    halo("send", 1)
     both(0, "middle")
     both(1, "middle")
+    halo("relay", 1)
     both(0, "gather1")
-    both(1, "start3")
-    halo("relay", 1)
+    both(1, "gather1")
+    halo("relay2", 0)
     both(0, "middle")
-    both(1, "gather3")
+    halo("relay2", 1)
+    both(1, "middle")
+    halo("relay2_y")
     attend(0)
-    both(1, "gather2")
     both(0, "end")
     learn(0)
-    both(1, "middle")
-    both(1, "gather1")
     attend(1)
-    both(1, "middle")
     both(1, "end")
     learn(1)
     for copy in outs.values():
@@ -454,7 +492,7 @@
 
 def per_device(queries, keys, values, w_gate, w_up, w_out):
     anywhere = pl.BlockSpec(memory_space=pl.ANY)
-    n_copies = 164
+    n_copies = 174
     wide, matrices = (2, HD, HD), (3, HD, HD)
     return pl.pallas_call(
         kernel,
@@ -469,7 +507,7 @@
             pltpu.VMEM((2,) + wide, BF16),
             pltpu.VMEM((2,) + wide, BF16),
             pltpu.VMEM((2,) + wide, BF16),
-            pltpu.VMEM(wide, BF16),
+            pltpu.VMEM((2,) + wide, BF16),
             pltpu.VMEM(wide, F32),
             pltpu.VMEM(wide, BF16),
             pltpu.VMEM(matrices, BF16),

time: 228 us -> 199 us (0.87)
  the two profiles are of different devices: /device:TPU:225 before, /device:TPU:1 now
where the time goes in v4:
time: 199 us
  Pallas kernels  197 us (99%)
  local copies, waits for them, and re-layouts  2.29 us (1%)
    pallas_call x1, Pallas kernels, per_device(): pl.pallas_call(kernel, out_shape=jax.ShapeDtypeStruct((128, 4096), BF16),...  197 us

profile of v4, /device:TPU:1, one launch (start us, length us, event | category | flops | bytes accessed | tf_op | source)
XLA Modules:
  0.0 199.3 jit_solution(1326213280526244155)
XLA Ops:
  0.0 197.0 %layer.1 = bf16[128,4096]{1,0:T(8,128)(2,1)} custom-call(bf16[128,4096]{1,0:T(8,128)(2,1)} %q_in.1, bf16[128,4096]{1,0:T(8,128)(2,1)} %k_in.1, bf16[128,4096]{1,0:T(8,128)(2,1)} %v_in.1, bf16[2,512,512]{2,1,0:T(8,128)(2,1)} %wg_in.1, bf16[2,512,512]{2,1,0:T(8,128)(2,1)} %wu_in.1, bf16[2,512,512]{2,1,0:T(8,128)(2,1)} %wo_in.1), custom_call_target="tpu_custom_call" | custom-call | tf_op jit(solution)/shard_map/layer/pallas_call | solution.py:497
  197.0 2.3 %copy.8 = bf16[128,4096]{1,0:T(8,128)(2,1)} copy(bf16[128,4096]{1,0:T(8,128)(2,1)} %layer.1) | data formatting | bytes 2097152

commit v5 on v4

--- a/solution.py
+++ b/solution.py
@@ -242,9 +242,8 @@
         self.source, self.last = (3, 0) if delta == 1 else (0, 3)
         self.x = x
         self.is_source, self.is_last = x == self.source, x == self.last
-        self.leaves_y, self.enters_y = z == self.source, z == self.last
-        ahead = lax.rem(z + delta + 4, 4)
-        onward = lax.select(self.enters_y, lax.rem(y + delta + 4, 4), y)
+        row = lax.rem(y * 4 + z + delta + 16, 16)
+        ahead = {Y: row // 4, Z: lax.rem(row, 4)}
         nearby = {X: lax.rem(x + delta + 4, 4)}
         every = slice(None)
         own = pl.ds(pl.multiple_of(hi * 256, 256), 256)
@@ -257,10 +256,9 @@
             if c != self.source:
                 self.leg1[c] = copies.make(piece, relays.at[0], {X: jnp.int32(c)})
                 piece = relays.at[0]
-            self.leg2[c] = copies.make(piece, relays.at[1], {Z: ahead})
-            if c == self.last:
-                self.short = copies.make(piece, end, {Z: ahead})
-            self.leg3[c] = copies.make(relays.at[1], end, {Y: onward, X: jnp.int32(self.last)})
+            self.leg2[c] = copies.make(piece, end if c == self.last else relays.at[1], ahead)
+            if c != self.last:
+                self.leg3[c] = copies.make(relays.at[1], end, {X: jnp.int32(self.last)})
 
     def send_early(self):
         pl.when(jnp.logical_not(self.is_source))(self.early.start)
@@ -274,44 +272,24 @@
                 if c != self.source:
                     self.leg1[c].start()
 
-    def second(self, c, step):
-        if c == self.last:
-            pl.when((self.x == c) & self.leaves_y)(lambda: getattr(self.leg2[c], step)())
-            pl.when((self.x == c) & jnp.logical_not(self.leaves_y))(lambda: getattr(self.short, step)())
-        else:
-            pl.when(self.x == c)(lambda: getattr(self.leg2[c], step)())
-
-    def third(self, c):
-        return (self.x == c) & self.enters_y if c == self.last else self.x == c
-
     def relay(self, h):
         for c in (2 * h, 2 * h + 1):
             if c != self.source:
                 pl.when(self.x == c)(self.leg1[c].wait_recv)
-            self.second(c, "start")
-
-    def forward(self, c, condition):
-        @pl.when((self.x == c) & condition)
-        def _():
-            self.leg2[c].wait_recv()
-            self.leg3[c].start()
+            pl.when(self.x == c)(self.leg2[c].start)
 
     def relay2(self, h):
         for c in (2 * h, 2 * h + 1):
             if c != self.last:
-                self.forward(c, jnp.logical_not(self.enters_y))
-
-    def relay2_y(self):
-        for c in range(4):
-            self.forward(c, self.enters_y)
+
+                @pl.when(self.x == c)
+                def _():
+                    self.leg2[c].wait_recv()
+                    self.leg3[c].start()
 
     def receive(self, h):
         for c in (2 * h, 2 * h + 1):
-            if c == self.last:
-                pl.when(self.is_last & self.enters_y)(self.leg3[c].wait_recv)
-                pl.when(self.is_last & jnp.logical_not(self.enters_y))(self.short.wait_recv)
-            else:
-                pl.when(self.is_last)(self.leg3[c].wait_recv)
+            pl.when(self.is_last)((self.leg2 if c == self.last else self.leg3)[c].wait_recv)
 
         @pl.when(jnp.logical_not(self.is_last))
         def _():
@@ -332,8 +310,9 @@
                 copy.wait_send()
 
         for c in range(4):
-            self.second(c, "wait_send")
-            pl.when(self.third(c))(self.leg3[c].wait_send)
+            pl.when(self.x == c)(self.leg2[c].wait_send)
+            if c != self.last:
+                pl.when(self.x == c)(self.leg3[c].wait_send)
 
 
 def kernel(
@@ -348,16 +327,10 @@
     partners = [{"head": p} for p in heads]
     for axis, offsets in ((X, (1, 2, 3)), (Y, (1, 3)), (Z, (1, 2, 3))):
         partners += [{axis: lax.rem(lax.axis_index(axis) + d, 4)} for d in offsets]
+    for d in (1, 3):
+        partners.append({axis: lax.rem(lax.axis_index(axis) + d, 4) for axis in (Y, Z)})
     for p in partners:
         pl.semaphore_signal(barrier, inc=1, device_id=p, device_id_type=MESH)
-    for corner, step in ((0, 3), (3, 1)):
-        above = {Y: lax.rem(lax.axis_index(Y) + step, 4)}
-
-        @pl.when(lax.axis_index(X) == corner)
-        def _():
-            for c in range(4):
-                pl.semaphore_signal(barrier, inc=1, device_id=above | {X: jnp.int32(c)}, device_id_type=MESH)
-
     def cols(p, h):
         return pl.ds(pl.multiple_of(p * 1024 + h * HD, HD), HD)
 
@@ -379,7 +352,7 @@
         stay(src, dst)
 
     copies = Copies(send_sem, recv_sem)
-    pl.semaphore_wait(barrier, len(partners) + 2)
+    pl.semaphore_wait(barrier, len(partners))
     sent = {}
 
     def send_pairs(h, js):
@@ -474,9 +447,8 @@
     both(1, "gather1")
     halo("relay2", 0)
     both(0, "middle")
+    both(1, "middle")
     halo("relay2", 1)
-    both(1, "middle")
-    halo("relay2_y")
     attend(0)
     both(0, "end")
     learn(0)

time: 199 us -> 189 us (0.950)
  the two profiles are of different devices: /device:TPU:1 before, /device:TPU:231 now
where the time goes in v5:
time: 189 us
  Pallas kernels  186 us (98%)
  local copies, waits for them, and re-layouts  2.29 us (1%)
    pallas_call x1, Pallas kernels, per_device(): pl.pallas_call(kernel, out_shape=jax.ShapeDtypeStruct((128, 4096), BF16),...  186 us

profile of v5, /device:TPU:231, one launch (start us, length us, event | category | flops | bytes accessed | tf_op | source)
XLA Modules:
  0.0 188.6 jit_solution(11478756572083494428)
XLA Ops:
  0.0 186.3 %layer.1 = bf16[128,4096]{1,0:T(8,128)(2,1)} custom-call(bf16[128,4096]{1,0:T(8,128)(2,1)} %q_in.1, bf16[128,4096]{1,0:T(8,128)(2,1)} %k_in.1, bf16[128,4096]{1,0:T(8,128)(2,1)} %v_in.1, bf16[2,512,512]{2,1,0:T(8,128)(2,1)} %wg_in.1, bf16[2,512,512]{2,1,0:T(8,128)(2,1)} %wu_in.1, bf16[2,512,512]{2,1,0:T(8,128)(2,1)} %wo_in.1), custom_call_target="tpu_custom_call" | custom-call | tf_op jit(solution)/shard_map/layer/pallas_call | solution.py:469
  186.3 2.3 %copy.8 = bf16[128,4096]{1,0:T(8,128)(2,1)} copy(bf16[128,4096]{1,0:T(8,128)(2,1)} %layer.1) | data formatting | bytes 2097152
